TPU v7x, 32 devices: a whole 2x2x4 slice. The times are simulated.
32 devices in a mesh: seq: 8 (over y, x, core), tp: 4 (over z).
Axes of the slice: x: 2, y: 2, z: 4, core: 2. Of those that a mesh axis runs over, the one named last changes fastest.
Arguments:
- queries: bfloat16 [4096, 8192], P('seq', 'tp'), may hold values from -6 to 6
- keys: bfloat16 [4096, 8192], P('seq', 'tp'), may hold values from -0.5 to 0.5
- values: bfloat16 [4096, 8192], P('seq', 'tp'), may hold values from -6 to 6
- gate: bfloat16 [4096, 8192], P('seq', 'tp'), may hold values from -6 to 6
- log_decay: float32 [4096, 64], P('seq', 'tp'), may hold values from -0.8 to 0
- out_grad: bfloat16 [4096, 8192], P('seq', 'tp'), may hold values from -6 to 6
Outputs:
- output: bfloat16 [4096, 8192], P('seq', 'tp')
- query_grad: bfloat16 [4096, 8192], P('seq', 'tp')
- key_grad: bfloat16 [4096, 8192], P('seq', 'tp')
- value_grad: bfloat16 [4096, 8192], P('seq', 'tp')
- gate_grad: bfloat16 [4096, 8192], P('seq', 'tp')
All inputs are finite; a program needn't handle non-finite values.
Results may differ from a plain program's by a relative error of at most 0.0051.
Values sent between devices are 32-bit elements; how exact they have to be, the bound alone decides.
A program may use at most 128 MiB of HBM per device.

v0:
```python
import functools

import jax
import jax.numpy as jnp
from jax import lax
from jax.experimental import pallas as pl
from jax.experimental.pallas import tpu as pltpu
from jax.sharding import PartitionSpec as P

MESH = pl.DeviceIdType.MESH
F32 = jnp.float32
BF16 = jnp.bfloat16
HIGH = lax.Precision.HIGHEST
EXTRA = 8
CHUNKS = 4


def nt(a, b):
    return lax.dot_general(a, b, (((1,), (1,)), ((), ())), preferred_element_type=F32)


def tn(a, b):
    return lax.dot_general(a, b, (((0,), (0,)), ((), ())), preferred_element_type=F32)


def nn(a, b):
    return lax.dot_general(a, b, (((1,), (0,)), ((), ())), preferred_element_type=F32)


def kernel(
    n_seq, n_tp, heads, dim, tokens,
    q_hbm, k_hbm, v_hbm, gate_hbm, rate_hbm, up_hbm,
    out_hbm, dq_hbm, dk_hbm, dv_hbm, gg_hbm,
    q, k, v, gate, rate, up, rates_wide, rows, cols, attn, dvp, grad, probs,
    own, other, sent, got, edge, far, state, sums, sums_in, scale_ref, center_ref,
    in_sem, out_sem, s0_send, s0_recv, st_send, st_recv, fin_send, fin_recv, tp_send, tp_recv,
):
    width = heads * dim * n_tp
    half = heads // 2
    bits = n_seq.bit_length() - 1
    chips = bits - 1
    per = half // CHUNKS
    block = min(256, tokens)
    nb = tokens // block
    me = lax.axis_index("seq")
    z = lax.axis_index("tp")
    core = lax.rem(me, 2)

    def bit_of(b):
        return lax.rem(me // (1 << b), 2)

    def partner(b):
        return (me + (1 << b) * (1 - 2 * bit_of(b)), z)

    def take(d, b):
        bit = bit_of(b).astype(F32)
        return bit if d == 0 else 1.0 - bit

    loads = []
    for i, (a, b) in enumerate(
        ((rate_hbm, rate), (k_hbm, k), (v_hbm, v), (q_hbm, q), (up_hbm, up), (gate_hbm, gate))
    ):
        c = pltpu.make_async_copy(a, b, in_sem.at[i])
        c.start()
        loads.append(c)

    barrier = pltpu.get_barrier_semaphore()
    for b in range(bits):
        pl.semaphore_signal(barrier, inc=1, device_id=partner(b), device_id_type=MESH)
    for d in range(1, n_tp):
        pl.semaphore_signal(
            barrier, inc=1, device_id=(me, lax.rem(z + d, n_tp)), device_id_type=MESH
        )

    def lane(h):
        return pl.ds(pl.multiple_of(h * dim, dim), dim)

    def pairs(body):
        @pl.loop(0, heads // 2)
        def _(i):
            body(2 * i)
            body(2 * i + 1)

    loads[0].wait()
    rates_wide[...] = jnp.zeros_like(rates_wide)
    rates_wide[0:heads, :] = rate[...]
    tri = (
        lax.broadcasted_iota(jnp.int32, (tokens, tokens), 0)
        >= lax.broadcasted_iota(jnp.int32, (tokens, tokens), 1)
    ).astype(F32)
    across = lax.dot_general(
        rates_wide[...], tri, (((1,), (1,)), ((), ())), precision=HIGH, preferred_element_type=F32
    )
    rows[...] = across
    within = across.T
    for h in range(heads):
        cols[h] = jnp.broadcast_to(within[:, h : h + 1], (tokens, dim))

    loads[1].wait()
    loads[2].wait()

    def make_local(h):
        last = cols[h, tokens - 1 : tokens, :]
        scaled = (k[:, lane(h)].astype(F32) * jnp.exp(last - cols[h])).astype(BF16)
        own[0, h, 0:dim, :] = tn(scaled, v[:, lane(h)])
        own[0, h, dim : dim + EXTRA, :] = jnp.broadcast_to(last, (EXTRA, dim))

    pairs(make_local)

    def s0_copy(d):
        return pltpu.make_async_remote_copy(
            src_ref=own.at[d], dst_ref=other.at[d], send_sem=s0_send.at[d],
            recv_sem=s0_recv.at[d], device_id=partner(0), device_id_type=MESH,
        )

    def st_copy(d, s, c):
        part = pl.ds(c * per, per)
        return pltpu.make_async_remote_copy(
            src_ref=sent.at[d, s, part], dst_ref=got.at[d, s, part], send_sem=st_send.at[d, s, c],
            recv_sem=st_recv.at[d, s, c], device_id=partner(s + 1), device_id_type=MESH,
        )

    def fin_copy(d, c):
        part = pl.ds(c * per, per)
        return pltpu.make_async_remote_copy(
            src_ref=edge.at[d, part], dst_ref=far.at[d, part], send_sem=fin_send.at[d, c],
            recv_sem=fin_recv.at[d, c], device_id=partner(0), device_id_type=MESH,
        )

    def joined(f, mine, theirs):
        dm, dt = mine[dim : dim + 1], theirs[dim : dim + 1]
        total = jnp.exp(dt * (1.0 - f)) * mine[0:dim] + jnp.exp(dm * f) * theirs[0:dim]
        return total, mine[dim:] + theirs[dim:]

    def step_first(d):
        s0_copy(d).wait_recv()
        f = take(d, 0)
        for c in range(CHUNKS):

            @pl.loop(0, per)
            def _(i):
                hh = c * per + i
                h = core * half + hh
                total, span = joined(f, own[d, h], other[d, h])
                sent[d, 0, hh, 0:dim, :] = total
                sent[d, 0, hh, dim:, :] = span
                edge[d, hh] = jnp.zeros((dim + EXTRA, dim), F32)

            if chips:
                st_copy(d, 0, c).start()
            else:
                fin_copy(d, c).start()

    def step(d, s, c):
        st_copy(d, s, c).wait_recv()
        f = take(d, s + 1)

        @pl.loop(0, per)
        def _(i):
            hh = c * per + i
            theirs = got[d, s, hh]
            e = edge[d, hh, dim : dim + 1, :]
            edge[d, hh, 0:dim, :] = edge[d, hh, 0:dim, :] + (f * jnp.exp(e)) * theirs[0:dim]
            edge[d, hh, dim:, :] = edge[d, hh, dim:, :] + f * theirs[dim:]
            if s + 1 < chips:
                total, span = joined(f, sent[d, s, hh], theirs)
                sent[d, s + 1, hh, 0:dim, :] = total
                sent[d, s + 1, hh, dim:, :] = span

        if s + 1 < chips:
            st_copy(d, s + 1, c).start()
        else:
            fin_copy(d, c).start()

    def step_last(d):
        f = take(d, 0)

        def put(h, e):
            span = other[d, h, dim : dim + 1, :]
            state[d, h] = (jnp.exp(span * f) * e + f * other[d, h, 0:dim, :]).astype(BF16)

        @pl.loop(0, half)
        def _(hh):
            put(core * half + hh, edge[d, hh, 0:dim, :])

        for c in range(CHUNKS):
            fin_copy(d, c).wait_recv()

            @pl.loop(0, per)
            def _(i):
                hh = c * per + i
                put((1 - core) * half + hh, far[d, hh, 0:dim, :])

    order = sorted(((s, c) for s in range(chips) for c in range(CHUNKS)), key=lambda p: (2 * p[0] + p[1], p[0]))

    def exchange_beside(d, body):
        trips = heads // 2
        s0_copy(d).start()
        early = min(2, trips)
        inside = order[: max(0, (trips - early) // 2)]

        @pl.loop(0, trips)
        def _(i):
            body(2 * i)
            body(2 * i + 1)

            @pl.when(i == early - 1)
            def _():
                step_first(d)

            for n, (s, c) in enumerate(inside):

                @pl.when(i == early + 2 * n + 1)
                def _():
                    step(d, s, c)

        for s, c in order[len(inside) :]:
            step(d, s, c)
        step_last(d)

    tiles = [(i, j) for i in range(nb) for j in range(i + 1)]
    keep = (
        lax.broadcasted_iota(jnp.int32, (block, block), 0)
        >= lax.broadcasted_iota(jnp.int32, (block, block), 1)
    )

    def decay_of(h, i, j):
        col = cols[h, i * block : (i + 1) * block, :]
        col = jnp.concatenate([col] * (block // dim), axis=1)
        row = rows[pl.ds(h, 1), j * block : (j + 1) * block]
        value = jnp.exp(jnp.minimum(col - row, 0.0))
        return jnp.where(keep, value, 0.0) if i == j else value

    def span_of(i):
        return slice(i * block, (i + 1) * block)

    def intra(h):
        for i in range(nb):
            total = None
            for j in range(i + 1):
                s = nt(q[span_of(i), lane(h)], k[span_of(j), lane(h)])
                p = (s * decay_of(h, i, j)).astype(BF16)
                probs[h, tiles.index((i, j))] = p
                o = nn(p, v[span_of(j), lane(h)])
                total = o if total is None else total + o
            attn[span_of(i), lane(h)] = total

    loads[3].wait()
    pl.semaphore_wait(barrier, bits + n_tp - 1)
    exchange_beside(0, intra)

    loads[4].wait()
    loads[5].wait()
    scale_ref[...] = jnp.zeros_like(scale_ref)
    center_ref[...] = jnp.zeros_like(center_ref)

    def finish_attn(h):
        for i in range(nb):
            r = span_of(i)
            a = attn[r, lane(h)] + jnp.exp(cols[h, r, :]) * nn(q[r, lane(h)], state[0, h])
            attn[r, lane(h)] = a
            scale_ref[r, :] = scale_ref[r, :] + a * a
            sig = jax.nn.sigmoid(gate[r, lane(h)].astype(F32))
            center_ref[r, :] = center_ref[r, :] + up[r, lane(h)].astype(F32) * sig * a

    pairs(finish_attn)

    ones = jnp.ones((8, dim), F32)

    def lanes_summed(x):
        return lax.dot_general(
            ones, x, (((1,), (1,)), ((), ())), precision=HIGH, preferred_element_type=F32
        )

    sums[0:8, :] = lanes_summed(scale_ref[...])
    sums[8:16, :] = lanes_summed(center_ref[...])

    def tp_copy(d):
        return pltpu.make_async_remote_copy(
            src_ref=sums, dst_ref=sums_in.at[d - 1], send_sem=tp_send.at[d - 1],
            recv_sem=tp_recv.at[d - 1], device_id=(me, lax.rem(z + d, n_tp)), device_id_type=MESH,
        )

    for d in range(1, n_tp):
        tp_copy(d).start()
    total = sums[...]
    for d in range(1, n_tp):
        tp_copy(d).wait_recv()
        total = total + sums_in[d - 1]

    def spread(x):
        return lax.dot_general(
            x, ones / 8.0, (((0,), (0,)), ((), ())), precision=HIGH, preferred_element_type=F32
        )

    scale = lax.rsqrt(spread(total[0:8]) / width + 1e-06)
    scale_ref[...] = scale
    center_ref[...] = spread(total[8:16]) * scale / width

    def pointwise(h):
        weighted = None
        for i in range(nb):
            r = span_of(i)
            sc = scale_ref[r, :]
            normed = attn[r, lane(h)] * sc
            sig = jax.nn.sigmoid(gate[r, lane(h)].astype(F32))
            dnorm = up[r, lane(h)].astype(F32) * sig
            g = (sc * (dnorm - normed * center_ref[r, :])).astype(BF16)
            grad[r, lane(h)] = g
            up[r, lane(h)] = (normed * sig).astype(BF16)
            gate[r, lane(h)] = (dnorm * normed * (1.0 - sig)).astype(BF16)
            grown = (q[r, lane(h)].astype(F32) * jnp.exp(cols[h, r, :])).astype(BF16)
            w = tn(grown, g)
            weighted = w if weighted is None else weighted + w
        own[1, h, 0:dim, :] = weighted
        own[1, h, dim : dim + EXTRA, :] = own[0, h, dim : dim + EXTRA, :]

    pairs(pointwise)

    outs = [
        pltpu.make_async_copy(a, b, out_sem.at[i])
        for i, (a, b) in enumerate(
            ((up, out_hbm), (gate, gg_hbm), (q, dq_hbm), (k, dk_hbm), (v, dv_hbm))
        )
    ]
    outs[0].start()
    outs[1].start()

    def backward(h):
        dq = [None] * nb
        dk = [None] * nb
        dv = [None] * nb

        def add(parts, n, x):
            parts[n] = x if parts[n] is None else parts[n] + x

        for i, j in tiles:
            g = grad[span_of(i), lane(h)]
            pg = (nt(g, v[span_of(j), lane(h)]) * decay_of(h, i, j)).astype(BF16)
            add(dq, i, nn(pg, k[span_of(j), lane(h)]))
            add(dk, j, tn(pg, q[span_of(i), lane(h)]))
            add(dv, j, tn(probs[h, tiles.index((i, j))], g))
        for i in range(nb):
            r = span_of(i)
            carried = jnp.exp(cols[h, r, :]) * nt(grad[r, lane(h)], state[0, h])
            q[r, lane(h)] = (dq[i] + carried).astype(BF16)
            attn[r, lane(h)] = dk[i]
            dvp[r, lane(h)] = dv[i]

    exchange_beside(1, backward)
    outs[2].start()

    def finish(h):
        last = cols[h, tokens - 1 : tokens, :]
        for i in range(nb):
            r = span_of(i)
            tail = jnp.exp(last - cols[h, r, :])
            kk, vv = k[r, lane(h)], v[r, lane(h)]
            dk = attn[r, lane(h)] + tail * nt(vv, state[1, h])
            dv = dvp[r, lane(h)] + tail * nn(kk, state[1, h])
            k[r, lane(h)] = dk.astype(BF16)
            v[r, lane(h)] = dv.astype(BF16)

    pairs(finish)
    outs[3].start()
    outs[4].start()

    for d in (0, 1):
        s0_copy(d).wait_send()
        for c in range(CHUNKS):
            for s in range(chips):
                st_copy(d, s, c).wait_send()
            fin_copy(d, c).wait_send()
    for d in range(1, n_tp):
        tp_copy(d).wait_send()
    for c in outs:
        c.wait()


def hand_on(*refs):
    for source, target in zip(refs[:5], refs[5:]):
        target[...] = source[...]


def solution(mesh):
    n_seq, n_tp = mesh.shape["seq"], mesh.shape["tp"]

    def shards(queries, keys, values, gate, log_decay, out_grad):
        tokens, flat = queries.shape
        heads = log_decay.shape[1]
        dim = flat // heads
        half = heads // 2
        chips = n_seq.bit_length() - 2
        block = min(256, tokens)
        nb = tokens // block
        big = pltpu.VMEM((tokens, flat), BF16)
        wide = pltpu.VMEM((tokens, flat), F32)
        message = (dim + EXTRA, dim)
        dma = pltpu.SemaphoreType.DMA
        any_spec = pl.BlockSpec(memory_space=pl.ANY)
        flops = 2 * tokens * tokens * flat * 5 + 2 * tokens * flat * dim * 7
        results = tuple(
            pl.pallas_call(
                functools.partial(kernel, n_seq, n_tp, heads, dim, tokens),
                out_shape=[jax.ShapeDtypeStruct((tokens, flat), BF16)] * 5,
                in_specs=[any_spec] * 6,
                out_specs=[any_spec] * 5,
                scratch_shapes=[
                    big, big, big, big, pltpu.VMEM((heads, tokens), F32), big,
                    pltpu.VMEM((128, tokens), F32), pltpu.VMEM((128, tokens), F32),
                    pltpu.VMEM((heads, tokens, dim), F32), wide, wide, big,
                    pltpu.VMEM((heads, nb * (nb + 1) // 2, block, block), BF16),
                    pltpu.VMEM((2, heads, *message), F32),
                    pltpu.VMEM((2, heads, *message), F32),
                    pltpu.VMEM((2, max(chips, 1), half, *message), F32),
                    pltpu.VMEM((2, max(chips, 1), half, *message), F32),
                    pltpu.VMEM((2, half, *message), F32),
                    pltpu.VMEM((2, half, *message), F32),
                    pltpu.VMEM((2, heads, dim, dim), BF16),
                    pltpu.VMEM((16, tokens), F32),
                    pltpu.VMEM((max(n_tp - 1, 1), 16, tokens), F32),
                    pltpu.VMEM((tokens, dim), F32), pltpu.VMEM((tokens, dim), F32),
                    dma((6,)), dma((5,)), dma((2,)), dma((2,)),
                    dma((2, max(chips, 1), CHUNKS)), dma((2, max(chips, 1), CHUNKS)),
                    dma((2, CHUNKS)), dma((2, CHUNKS)),
                    dma((max(n_tp - 1, 1),)), dma((max(n_tp - 1, 1),)),
                ],
                compiler_params=pltpu.CompilerParams(
                    collective_id=0, has_side_effects=True, vmem_limit_bytes=58 << 20
                ),
                cost_estimate=pl.CostEstimate(
                    flops=flops, bytes_accessed=tokens * flat * 20, transcendentals=0
                ),
            )(queries, keys, values, gate, log_decay.T, out_grad)
        )
        strip = pl.BlockSpec((tokens, flat // 4), lambda i: (0, i))
        return tuple(
            pl.pallas_call(
                hand_on,
                grid=(4,),
                out_shape=[jax.ShapeDtypeStruct((tokens, flat), BF16)] * 5,
                in_specs=[strip] * 5,
                out_specs=[strip] * 5,
            )(*results)
        )

    spec = P("seq", "tp")
    return jax.shard_map(
        shards, mesh=mesh, in_specs=(spec,) * 6, out_specs=(spec,) * 5, check_vma=False
    )
```

profile of v0, /device:TPU:0, one launch (start us, length us, event | category | flops | bytes accessed | tf_op | source)
XLA Modules:
  0.0 83.9 jit_solution(3514637984565778496)
XLA Ops:
  0.6 75.1 %shard_map.101 = (bf16[512,2048]{1,0:T(8,128)(2,1)}, bf16[512,2048]{1,0:T(8,128)(2,1)}, bf16[512,2048]{1,0:T(8,128)(2,1)}, bf16[512,2048]{1,0:T(8,128)(2,1)}, bf16[512,2048]{1,0:T(8,128)(2,1)}) custom-call(bf16[512,2048]{1,0:T(8,128)(2,1)} %q_hbm.1, bf16[512,2048]{1,0:T(8,128)(2,1)} %k_hbm.1, bf16[512,2048]{1,0:T(8,128)(2,1)} %v_hbm.1, ...), custom_call_target="tpu_custom_call" | custom-call | flops 7247757312 | bytes 20971520 | tf_op jit(solution)/shard_map/pallas_call | solution.py:403
  75.8 8.1 %shard_map.102 = (bf16[512,2048]{1,0:T(8,128)(2,1)}, bf16[512,2048]{1,0:T(8,128)(2,1)}, bf16[512,2048]{1,0:T(8,128)(2,1)}, bf16[512,2048]{1,0:T(8,128)(2,1)}, bf16[512,2048]{1,0:T(8,128)(2,1)}) custom-call(bf16[512,2048]{1,0:T(8,128)(2,1)} %get-tuple-element.10.refs_0_, bf16[512,2048]{1,0:T(8,128)(2,1)} %get-tuple-element.11.refs_1_, ...), custom_call_target="tpu_custom_call" | custom-call | tf_op jit(solution)/shard_map/pallas_call | solution.py:438
where the time goes:
time: 84.6 us; the launch traced here: 83.9 us
  Pallas kernels  83.3 us (98%)
    pallas_call x1, Pallas kernels, shards(): pl.pallas_call(functools.partial(kernel, n_seq, n_tp, heads, dim, tokens)...  75.1 us
    pallas_call x1, Pallas kernels, shards(): pl.pallas_call(hand_on, grid=(4,), out_shape=[jax.ShapeDtypeStruct((token...  8.13 us

commit v1 on v0

v1 whole, which is shorter than its diff:
```python
import functools

import jax
import jax.numpy as jnp
from jax import lax
from jax.experimental import pallas as pl
from jax.experimental.pallas import tpu as pltpu
from jax.sharding import PartitionSpec as P

MESH = pl.DeviceIdType.MESH
F32 = jnp.float32
BF16 = jnp.bfloat16


def nt(a, b):
    return lax.dot_general(a, b, (((1,), (1,)), ((), ())), preferred_element_type=F32)


def tn(a, b):
    return lax.dot_general(a, b, (((0,), (0,)), ((), ())), preferred_element_type=F32)


def nn(a, b):
    return lax.dot_general(a, b, (((1,), (0,)), ((), ())), preferred_element_type=F32)


def three_parts(x):
    high = x.astype(BF16).astype(F32)
    rest = x - high
    middle = rest.astype(BF16).astype(F32)
    low = (rest - middle).astype(BF16).astype(F32)
    return high, middle, low


def stacked(x):
    parts = three_parts(x)
    spare = 128 - 3 * x.shape[0]
    return jnp.concatenate([*parts, jnp.zeros((spare, x.shape[1]), F32)], axis=0)


def kernel(
    n_seq, n_tp, heads, dim, tokens,
    q_hbm, k_hbm, v_hbm, gate_hbm, rate_hbm, up_hbm,
    up, gate, q, k, v, attn, dvp, state_grad, cols,
    rate, rows, split, grad, probs,
    own, other, sent, got, edge, far, state, span, span_in, factor,
    sums, sums_in, scale_ref, center_ref,
    in_sem, sp_send, sp_recv, s0_send, s0_recv, st_send, st_recv, fin_send, fin_recv, tp_send, tp_recv,
):
    width = heads * dim * n_tp
    half = heads // 2
    bits = n_seq.bit_length() - 1
    chips = bits - 1
    block = min(256, tokens)
    nb = tokens // block
    me = lax.axis_index("seq")
    z = lax.axis_index("tp")
    core = lax.rem(me, 2)

    def bit_of(b):
        return lax.rem(me // (1 << b), 2)

    def partner(b):
        return (me + (1 << b) * (1 - 2 * bit_of(b)), z)

    def takes(d, b):
        return bit_of(b) if d == 0 else 1 - bit_of(b)

    def load(i, a, b):
        return pltpu.make_async_copy(a, b, in_sem.at[i])

    loads = [
        load(i, a, b)
        for i, (a, b) in enumerate(
            ((rate_hbm, rate), (k_hbm, k), (v_hbm, v), (q_hbm, q), (up_hbm, up), (gate_hbm, gate))
        )
    ]
    for c in loads[:3]:
        c.start()

    barrier = pltpu.get_barrier_semaphore()
    for b in range(bits):
        pl.semaphore_signal(barrier, inc=1, device_id=partner(b), device_id_type=MESH)
    for d in range(1, n_tp):
        pl.semaphore_signal(
            barrier, inc=1, device_id=(me, lax.rem(z + d, n_tp)), device_id_type=MESH
        )

    def lane(h):
        return pl.ds(pl.multiple_of(h * dim, dim), dim)

    def mine(c):
        return core * half + c

    def others(c):
        return (1 - core) * half + c

    loads[0].wait()
    upto = (
        lax.broadcasted_iota(jnp.int32, (tokens, tokens), 0)
        <= lax.broadcasted_iota(jnp.int32, (tokens, tokens), 1)
    ).astype(BF16)
    parts = nn(stacked(rate[...]).astype(BF16), upto)
    across = parts[0:heads] + parts[heads : 2 * heads] + parts[2 * heads : 3 * heads]
    rows[...] = across
    split[...] = stacked(across).T.astype(BF16)
    span[0] = jnp.broadcast_to(across[:, tokens - 1 : tokens], (heads, dim))
    loads[3].start()
    pl.semaphore_wait(barrier, bits + n_tp - 1)

    def sp_copy(b):
        return pltpu.make_async_remote_copy(
            src_ref=span.at[b], dst_ref=span_in.at[b], send_sem=sp_send.at[b],
            recv_sem=sp_recv.at[b], device_id=partner(b), device_id_type=MESH,
        )

    sp_copy(0).start()

    def s0_copy(d, h):
        return pltpu.make_async_remote_copy(
            src_ref=own.at[d, h], dst_ref=other.at[d, h], send_sem=s0_send.at[d, h],
            recv_sem=s0_recv.at[d, h], device_id=partner(0), device_id_type=MESH,
        )

    def st_copy(d, s, c):
        return pltpu.make_async_remote_copy(
            src_ref=sent.at[d, s, c], dst_ref=got.at[d, s, c], send_sem=st_send.at[d, s, c],
            recv_sem=st_recv.at[d, s, c], device_id=partner(s + 1), device_id_type=MESH,
        )

    def fin_copy(d, c):
        return pltpu.make_async_remote_copy(
            src_ref=edge.at[d, c], dst_ref=far.at[d, c], send_sem=fin_send.at[d, c],
            recv_sem=fin_recv.at[d, c], device_id=partner(0), device_id_type=MESH,
        )

    def span_step(b):
        sp_copy(b).wait_recv()
        here, there = span[b], span_in[b]
        if b + 1 < bits:
            span[b + 1] = here + there
            sp_copy(b + 1).start()
        for d in (0, 1):
            f = takes(d, b).astype(F32)
            factor[d, b, 0] = jnp.exp(there * (1.0 - f))
            factor[d, b, 1] = jnp.exp(here * f)
            if b == 0:
                factor[d, b, 2] = jnp.exp(there * f)
            else:
                before = jnp.zeros((heads, dim), F32)
                for r in range(1, b):
                    before = before + takes(d, r).astype(F32) * span_in[r]
                factor[d, b, 2] = f * jnp.exp(before)

    def row_of(d, b, n, h):
        return factor[d, b, n, pl.ds(h, 1), :]

    def send_level(d, s, c):
        if s == chips - 1:

            @pl.when(takes(d, s + 1) == 0)
            def _():
                st_copy(d, s, c).start()
        else:
            st_copy(d, s, c).start()

    def level0(d, c):
        h = mine(c)
        s0_copy(d, h).wait_recv()
        sent[d, 0, c] = row_of(d, 0, 0, h) * own[d, h] + row_of(d, 0, 1, h) * other[d, h]
        send_level(d, 0, c)

    def step(d, s, c):
        h = mine(c)

        def arrive():
            st_copy(d, s, c).wait_recv()
            theirs = got[d, s, c]
            on_top = row_of(d, s + 1, 2, h) * theirs
            edge[d, c] = on_top if s == 0 else edge[d, c] + on_top
            if s + 1 < chips:
                sent[d, s + 1, c] = (
                    row_of(d, s + 1, 0, h) * sent[d, s, c] + row_of(d, s + 1, 1, h) * theirs
                )

        if s + 1 < chips:
            arrive()
            send_level(d, s + 1, c)
            return
        pl.when(takes(d, s + 1) == 1)(arrive)
        if s == 0:

            @pl.when(takes(d, s + 1) == 0)
            def _():
                edge[d, c] = jnp.zeros((dim, dim), F32)

        fin_copy(d, c).start()

    def put(d, c, target):
        f = takes(d, 0).astype(F32)
        h = mine(c)
        target[h] = (row_of(d, 0, 2, h) * edge[d, c] + f * other[d, h]).astype(BF16)
        h = others(c)
        s0_copy(d, h).wait_recv()
        fin_copy(d, c).wait_recv()
        target[h] = (row_of(d, 0, 2, h) * far[d, c] + f * other[d, h]).astype(BF16)

    def local_pair(c):
        pair = (others(c), mine(c))
        at = lax.broadcasted_iota(jnp.int32, (128, dim), 0)
        pick = jnp.concatenate(
            [
                ((at == h) | (at == h + heads) | (at == h + 2 * heads)).astype(F32).astype(BF16)
                for h in pair
            ],
            axis=1,
        )
        wide = nn(split[...], pick)
        for n, h in enumerate(pair):
            col = wide[:, n * dim : (n + 1) * dim]
            cols[h] = col
            last = col[tokens - 1 : tokens, :]
            scaled = (k[:, lane(h)].astype(F32) * jnp.exp(last - col)).astype(BF16)
            own[0, h] = tn(scaled, v[:, lane(h)])
        for h in pair:
            s0_copy(0, h).start()

    def first_exchange(d, body, lead):
        lead = min(lead, half)

        @pl.loop(0, lead)
        def _(c):
            body(c)

        if d == 0:
            span_step(0)

        @pl.loop(lead, half)
        def _(c):
            body(c)
            level0(d, c - lead)

        if d == 0:
            for b in range(1, bits):
                span_step(b)

        @pl.loop(half - lead, half)
        def _(c):
            level0(d, c)

    def ticks(d, body, early, finish):
        lags = [2 * s - early for s in range(chips)]
        lag = lags[-1] + 1
        for s in range(chips):
            for c in range(max(0, -lags[s])):
                step(d, s, c)

        @pl.loop(0, half + lag)
        def _(t):
            @pl.when(t < half)
            def _():
                body(t)

            for s in range(chips):

                @pl.when((t >= max(0, lags[s])) & (t < half + lags[s]))
                def _():
                    step(d, s, t - lags[s])

            @pl.when(t >= lag)
            def _():
                finish(t - lag)

    loads[1].wait()
    loads[2].wait()
    first_exchange(0, local_pair, 3)
    loads[4].start()
    loads[5].start()

    tiles = [(i, j) for i in range(nb) for j in range(i + 1)]
    keep = (
        lax.broadcasted_iota(jnp.int32, (block, block), 0)
        >= lax.broadcasted_iota(jnp.int32, (block, block), 1)
    )

    def decay_of(h, i, j):
        col = cols[h, i * block : (i + 1) * block, :]
        col = jnp.concatenate([col] * (block // dim), axis=1)
        row = rows[pl.ds(h, 1), j * block : (j + 1) * block]
        value = jnp.exp(jnp.minimum(col - row, 0.0))
        return jnp.where(keep, value, 0.0) if i == j else value

    def span_of(i):
        return slice(i * block, (i + 1) * block)

    def intra(h):
        for i in range(nb):
            total = None
            for j in range(i + 1):
                s = nt(q[span_of(i), lane(h)], k[span_of(j), lane(h)])
                p = (s * decay_of(h, i, j)).astype(BF16)
                probs[h, tiles.index((i, j))] = p
                o = nn(p, v[span_of(j), lane(h)])
                total = o if total is None else total + o
            attn[span_of(i), lane(h)] = total

    def both(body):
        def pair(c):
            body(mine(c))
            body(others(c))

        return pair

    def finish_attn(c):
        put(0, c, state)
        for i in range(nb):
            r = span_of(i)
            square, inner = scale_ref[r, :], center_ref[r, :]
            for h in (mine(c), others(c)):
                a = attn[r, lane(h)] + jnp.exp(cols[h, r, :]) * nn(q[r, lane(h)], state[h])
                attn[r, lane(h)] = a
                square = square + a * a
                sig = jax.nn.sigmoid(gate[r, lane(h)].astype(F32))
                inner = inner + up[r, lane(h)].astype(F32) * sig * a
            scale_ref[r, :] = square
            center_ref[r, :] = inner

    scale_ref[...] = jnp.zeros_like(scale_ref)
    center_ref[...] = jnp.zeros_like(center_ref)
    loads[3].wait()
    loads[4].wait()
    loads[5].wait()
    ticks(0, both(intra), 0, finish_attn)

    strips = tokens // 128

    def packed(x):
        turned = jnp.sum(x.T, axis=0, keepdims=True)
        return [turned[:, n * 128 : (n + 1) * 128] for n in range(strips)]

    spare = -2 * strips % 8
    pieces = packed(scale_ref[...]) + packed(center_ref[...])
    if spare:
        pieces.append(jnp.zeros((spare, 128), F32))
    sums[...] = jnp.concatenate(pieces, axis=0)

    def tp_copy(d):
        return pltpu.make_async_remote_copy(
            src_ref=sums, dst_ref=sums_in.at[d - 1], send_sem=tp_send.at[d - 1],
            recv_sem=tp_recv.at[d - 1], device_id=(me, lax.rem(z + d, n_tp)), device_id_type=MESH,
        )

    for d in range(1, n_tp):
        tp_copy(d).start()
    total = sums[...]
    for d in range(1, n_tp):
        tp_copy(d).wait_recv()
        total = total + sums_in[d - 1]
    scale = lax.rsqrt(total[0:strips] / width + 1e-06)
    center = total[strips : 2 * strips] * scale / width
    for n in range(strips):
        r = slice(n * 128, (n + 1) * 128)
        scale_ref[r, :] = jnp.broadcast_to(scale[n : n + 1, :], (128, 128)).T
        center_ref[r, :] = jnp.broadcast_to(center[n : n + 1, :], (128, 128)).T

    def pointwise(h):
        weighted = None
        for i in range(nb):
            r = span_of(i)
            sc = scale_ref[r, :]
            normed = attn[r, lane(h)] * sc
            sig = jax.nn.sigmoid(gate[r, lane(h)].astype(F32))
            dnorm = up[r, lane(h)].astype(F32) * sig
            g = (sc * (dnorm - normed * center_ref[r, :])).astype(BF16)
            grad[r, lane(h)] = g
            up[r, lane(h)] = (normed * sig).astype(BF16)
            gate[r, lane(h)] = (dnorm * normed * (1.0 - sig)).astype(BF16)
            grown = (q[r, lane(h)].astype(F32) * jnp.exp(cols[h, r, :])).astype(BF16)
            w = tn(grown, g)
            weighted = w if weighted is None else weighted + w
        own[1, h] = weighted

    def pointwise_pair(c):
        pair = (others(c), mine(c))
        for h in pair:
            pointwise(h)
        for h in pair:
            s0_copy(1, h).start()

    first_exchange(1, pointwise_pair, 3)

    def backward(h):
        dq = [None] * nb
        dk = [None] * nb
        dv = [None] * nb

        def add(parts, n, x):
            parts[n] = x if parts[n] is None else parts[n] + x

        for i, j in tiles:
            g = grad[span_of(i), lane(h)]
            pg = (nt(g, v[span_of(j), lane(h)]) * decay_of(h, i, j)).astype(BF16)
            add(dq, i, nn(pg, k[span_of(j), lane(h)]))
            add(dk, j, tn(pg, q[span_of(i), lane(h)]))
            add(dv, j, tn(probs[h, tiles.index((i, j))], g))
        for i in range(nb):
            r = span_of(i)
            carried = jnp.exp(cols[h, r, :]) * nt(grad[r, lane(h)], state[h])
            q[r, lane(h)] = (dq[i] + carried).astype(BF16)
            attn[r, lane(h)] = dk[i]
            dvp[r, lane(h)] = dv[i]

    ticks(1, both(backward), 1, lambda c: put(1, c, state_grad))

    for b in range(bits):
        sp_copy(b).wait_send()
    for d in (0, 1):

        @pl.loop(0, heads)
        def _(h):
            s0_copy(d, h).wait_send()

        @pl.loop(0, half)
        def _(c):
            for s in range(chips - 1):
                st_copy(d, s, c).wait_send()

            @pl.when(takes(d, chips) == 0)
            def _():
                st_copy(d, chips - 1, c).wait_send()

            fin_copy(d, c).wait_send()

    for d in range(1, n_tp):
        tp_copy(d).wait_send()


def last_kernel(
    heads, dim, tokens,
    out_ref, gg_ref, dq_ref, k, v, dkp, dvp, state_grad, cols,
    out_hbm, dq_hbm, dk_hbm, dv_hbm, gg_hbm,
    dk, dv, sem, pair_sem,
):
    block = min(256, tokens)
    trips = heads // 2
    whole = [
        pltpu.make_async_copy(a, b, sem.at[i])
        for i, (a, b) in enumerate(((out_ref, out_hbm), (gg_ref, gg_hbm), (dq_ref, dq_hbm)))
    ]
    for c in whole:
        c.start()

    def strips(i):
        part = pl.ds(pl.multiple_of(i * 2 * dim, 2 * dim), 2 * dim)
        return [
            pltpu.make_async_copy(a.at[:, part], b.at[:, part], pair_sem.at[n, i])
            for n, (a, b) in enumerate(((dk, dk_hbm), (dv, dv_hbm)))
        ]

    @pl.loop(0, trips)
    def _(i):
        for h in (2 * i, 2 * i + 1):
            at = pl.ds(pl.multiple_of(h * dim, dim), dim)
            last = cols[h, tokens - 1 : tokens, :]
            for n in range(tokens // block):
                r = slice(n * block, (n + 1) * block)
                tail = jnp.exp(last - cols[h, r, :])
                key = dkp[r, at] + tail * nt(v[r, at], state_grad[h])
                value = dvp[r, at] + tail * nn(k[r, at], state_grad[h])
                dk[r, at] = key.astype(BF16)
                dv[r, at] = value.astype(BF16)
        for c in strips(i):
            c.start()

    @pl.loop(0, trips)
    def _(i):
        for c in strips(i):
            c.wait()

    for c in whole:
        c.wait()


def solution(mesh):
    n_seq, n_tp = mesh.shape["seq"], mesh.shape["tp"]

    def shards(queries, keys, values, gate, log_decay, out_grad):
        tokens, flat = queries.shape
        heads = log_decay.shape[1]
        dim = flat // heads
        half = heads // 2
        bits = n_seq.bit_length() - 1
        chips = bits - 1
        block = min(256, tokens)
        nb = tokens // block
        tile = (dim, dim)
        dma = pltpu.SemaphoreType.DMA
        peers = max(n_tp - 1, 1)
        sums = (-(-2 * (tokens // 128) // 8) * 8, 128)
        hbm = pl.BlockSpec(memory_space=pltpu.HBM)
        vmem = pl.BlockSpec(memory_space=pltpu.VMEM)
        big = pltpu.VMEM((tokens, flat), BF16)
        wide = pltpu.VMEM((tokens, flat), F32)
        flops = 2 * tokens * tokens * flat * 5 + 2 * tokens * flat * dim * 7
        up, gg, dq, k, v, dkp, dvp, state_grad, cols = pl.pallas_call(
            functools.partial(kernel, n_seq, n_tp, heads, dim, tokens),
            out_shape=[
                big, big, big, big, big, wide, wide,
                pltpu.VMEM((heads, *tile), BF16), pltpu.VMEM((heads, tokens, dim), F32),
            ],
            in_specs=[hbm] * 6,
            out_specs=[vmem] * 9,
            scratch_shapes=[
                pltpu.VMEM((heads, tokens), F32), pltpu.VMEM((heads, tokens), F32),
                pltpu.VMEM((tokens, 128), BF16), big,
                pltpu.VMEM((heads, nb * (nb + 1) // 2, block, block), BF16),
                pltpu.VMEM((2, heads, *tile), F32),
                pltpu.VMEM((2, heads, *tile), F32),
                pltpu.VMEM((2, chips, half, *tile), F32),
                pltpu.VMEM((2, chips, half, *tile), F32),
                pltpu.VMEM((2, half, *tile), F32),
                pltpu.VMEM((2, half, *tile), F32),
                pltpu.VMEM((heads, *tile), BF16),
                pltpu.VMEM((bits, heads, dim), F32), pltpu.VMEM((bits, heads, dim), F32),
                pltpu.VMEM((2, bits, 3, heads, dim), F32),
                pltpu.VMEM(sums, F32), pltpu.VMEM((peers, *sums), F32),
                pltpu.VMEM((tokens, dim), F32), pltpu.VMEM((tokens, dim), F32),
                dma((6,)), dma((bits,)), dma((bits,)), dma((2, heads)), dma((2, heads)),
                dma((2, chips, half)), dma((2, chips, half)), dma((2, half)), dma((2, half)),
                dma((peers,)), dma((peers,)),
            ],
            compiler_params=pltpu.CompilerParams(
                collective_id=0, has_side_effects=True, vmem_limit_bytes=36 << 20
            ),
            cost_estimate=pl.CostEstimate(
                flops=flops, bytes_accessed=tokens * flat * 10, transcendentals=0
            ),
        )(queries, keys, values, gate, log_decay.T, out_grad)
        return tuple(
            pl.pallas_call(
                functools.partial(last_kernel, heads, dim, tokens),
                out_shape=[jax.ShapeDtypeStruct((tokens, flat), BF16)] * 5,
                in_specs=[vmem] * 9,
                out_specs=[hbm] * 5,
                scratch_shapes=[big, big, dma((3,)), dma((2, half))],
                compiler_params=pltpu.CompilerParams(vmem_limit_bytes=16 << 20),
                cost_estimate=pl.CostEstimate(
                    flops=4 * tokens * flat * dim, bytes_accessed=tokens * flat * 10, transcendentals=0
                ),
            )(up, gg, dq, k, v, dkp, dvp, state_grad, cols)
        )

    spec = P("seq", "tp")
    return jax.shard_map(
        shards, mesh=mesh, in_specs=(spec,) * 6, out_specs=(spec,) * 5, check_vma=False
    )
```

time: 84.6 us -> 66 us (0.78)
  Pallas kernels: 83.3 us -> 65 us
    pallas_call x1, Pallas kernels: 75.1 us -> 60.9 us  [shards(): pl.pallas_call(functools.partial(kernel, n_seq, n_tp, heads, dim, tokens)...]
    pallas_call x1, Pallas kernels: 8.13 us -> 4.07 us  [shards(): pl.pallas_call(functools.partial(last_kernel, heads, dim, tokens), out_sh...]
where the time goes in v1:
time: 66 us; the launch traced here: 65.6 us
  Pallas kernels  65 us (98%)
    pallas_call x1, Pallas kernels, shards(): pl.pallas_call(functools.partial(kernel, n_seq, n_tp, heads, dim, tokens)...  60.9 us
    pallas_call x1, Pallas kernels, shards(): pl.pallas_call(functools.partial(last_kernel, heads, dim, tokens), out_sh...  4.07 us

profile of v1, /device:TPU:0, one launch (start us, length us, event | category | flops | bytes accessed | tf_op | source)
XLA Modules:
  0.0 65.6 jit_solution(1692324417703510814)
XLA Ops:
  0.6 60.9 %shard_map.101 = (bf16[512,2048]{1,0:T(8,128)(2,1)S(1)}, bf16[512,2048]{1,0:T(8,128)(2,1)S(1)}, bf16[512,2048]{1,0:T(8,128)(2,1)S(1)}, bf16[512,2048]{1,0:T(8,12...) custom-call(bf16[512,2048]{1,0:T(8,128)(2,1)} %q_hbm.1, ...), custom_call_target="tpu_custom_call" | custom-call | flops 7247757312 | bytes 10485760 | tf_op jit(solution)/shard_map/pallas_call | solution.py:505
  61.6 4.1 %shard_map.102 = (bf16[512,2048]{1,0:T(8,128)(2,1)}, bf16[512,2048]{1,0:T(8,128)(2,1)}, bf16[512,2048]{1,0:T(8,128)(2,1)}, bf16[512,2048]{1,0:T(8,128)(2,1)}, bf16[512,2048]{1,0:T(8,128)(2,1)}) custom-call(bf16[512,2048]{1,0:T(8,128)(2,1)S(1)} %get-tuple-element.14.out_ref, bf16[512,2048]{1,0:T(8,128)(2,1)S(1)} %get-tuple-element.15.gg_ref, ...), custom_call_target="tpu_custom_call" | custom-call | flops 536870912 | bytes 10485760 | tf_op jit(solution)/shard_map/pallas_call | solution.py:540

commit v2 on v1

--- a/solution.py
+++ b/solution.py
@@ -10,6 +10,8 @@
 MESH = pl.DeviceIdType.MESH
 F32 = jnp.float32
 BF16 = jnp.bfloat16
+LOG2E = 1.4426950408889634
+LOW = -1e9
 
 
 def nt(a, b):
@@ -41,8 +43,8 @@
 def kernel(
     n_seq, n_tp, heads, dim, tokens,
     q_hbm, k_hbm, v_hbm, gate_hbm, rate_hbm, up_hbm,
-    up, gate, q, k, v, attn, dvp, state_grad, cols,
-    rate, rows, split, grad, probs,
+    up, gate, grown, k, v, dkt, dvt, state_grad, rows,
+    rate, q, cols, split, bias, inside, attn, sig, dnorm, grad, probs,
     own, other, sent, got, edge, far, state, span, span_in, factor,
     sums, sums_in, scale_ref, center_ref,
     in_sem, sp_send, sp_recv, s0_send, s0_recv, st_send, st_recv, fin_send, fin_recv, tp_send, tp_recv,
@@ -102,10 +104,32 @@
     ).astype(BF16)
     parts = nn(stacked(rate[...]).astype(BF16), upto)
     across = parts[0:heads] + parts[heads : 2 * heads] + parts[2 * heads : 3 * heads]
+    across = across * LOG2E
     rows[...] = across
     split[...] = stacked(across).T.astype(BF16)
     span[0] = jnp.broadcast_to(across[:, tokens - 1 : tokens], (heads, dim))
     loads[3].start()
+    corner = lax.broadcasted_iota(jnp.int32, (dim, dim), 0) >= lax.broadcasted_iota(
+        jnp.int32, (dim, dim), 1
+    )
+    bias[...] = jnp.where(corner, 0.0, LOW)
+
+    @pl.loop(0, half)
+    def _(i):
+        pair = (2 * i, 2 * i + 1)
+        at = lax.broadcasted_iota(jnp.int32, (128, dim), 0)
+        pick = jnp.concatenate(
+            [
+                ((at == h) | (at == h + heads) | (at == h + 2 * heads)).astype(F32).astype(BF16)
+                for h in pair
+            ],
+            axis=1,
+        )
+        for r in (slice(n, n + 256) for n in range(0, tokens, 256)):
+            wide = nn(split[r, :], pick)
+            for n, h in enumerate(pair):
+                cols[h, r, :] = wide[:, n * dim : (n + 1) * dim]
+
     pl.semaphore_wait(barrier, bits + n_tp - 1)
 
     def sp_copy(b):
@@ -118,19 +142,19 @@
 
     def s0_copy(d, h):
         return pltpu.make_async_remote_copy(
-            src_ref=own.at[d, h], dst_ref=other.at[d, h], send_sem=s0_send.at[d, h],
+            src_ref=own.at[d, h], dst_ref=other.at[d, h], send_sem=s0_send.at[d],
             recv_sem=s0_recv.at[d, h], device_id=partner(0), device_id_type=MESH,
         )
 
     def st_copy(d, s, c):
         return pltpu.make_async_remote_copy(
-            src_ref=sent.at[d, s, c], dst_ref=got.at[d, s, c], send_sem=st_send.at[d, s, c],
+            src_ref=sent.at[d, s, c], dst_ref=got.at[d, s, c], send_sem=st_send.at[d, s],
             recv_sem=st_recv.at[d, s, c], device_id=partner(s + 1), device_id_type=MESH,
         )
 
     def fin_copy(d, c):
         return pltpu.make_async_remote_copy(
-            src_ref=edge.at[d, c], dst_ref=far.at[d, c], send_sem=fin_send.at[d, c],
+            src_ref=edge.at[d, c], dst_ref=far.at[d, c], send_sem=fin_send.at[d],
             recv_sem=fin_recv.at[d, c], device_id=partner(0), device_id_type=MESH,
         )
 
@@ -142,15 +166,15 @@
             sp_copy(b + 1).start()
         for d in (0, 1):
             f = takes(d, b).astype(F32)
-            factor[d, b, 0] = jnp.exp(there * (1.0 - f))
-            factor[d, b, 1] = jnp.exp(here * f)
+            factor[d, b, 0] = jnp.exp2(there * (1.0 - f))
+            factor[d, b, 1] = jnp.exp2(here * f)
             if b == 0:
-                factor[d, b, 2] = jnp.exp(there * f)
+                factor[d, b, 2] = jnp.exp2(there * f)
             else:
                 before = jnp.zeros((heads, dim), F32)
                 for r in range(1, b):
                     before = before + takes(d, r).astype(F32) * span_in[r]
-                factor[d, b, 2] = f * jnp.exp(before)
+                factor[d, b, 2] = f * jnp.exp2(before)
 
     def row_of(d, b, n, h):
         return factor[d, b, n, pl.ds(h, 1), :]
@@ -207,21 +231,12 @@
 
     def local_pair(c):
         pair = (others(c), mine(c))
-        at = lax.broadcasted_iota(jnp.int32, (128, dim), 0)
-        pick = jnp.concatenate(
-            [
-                ((at == h) | (at == h + heads) | (at == h + 2 * heads)).astype(F32).astype(BF16)
-                for h in pair
-            ],
-            axis=1,
-        )
-        wide = nn(split[...], pick)
-        for n, h in enumerate(pair):
-            col = wide[:, n * dim : (n + 1) * dim]
-            cols[h] = col
-            last = col[tokens - 1 : tokens, :]
-            scaled = (k[:, lane(h)].astype(F32) * jnp.exp(last - col)).astype(BF16)
-            own[0, h] = tn(scaled, v[:, lane(h)])
+        scaled = []
+        for h in pair:
+            last = cols[h, tokens - 1 : tokens, :]
+            scaled.append((k[:, lane(h)].astype(F32) * jnp.exp2(last - cols[h])).astype(BF16))
+        for h, x in zip(pair, scaled):
+            own[0, h] = tn(x, v[:, lane(h)])
         for h in pair:
             s0_copy(0, h).start()
 
@@ -278,38 +293,66 @@
     loads[5].start()
 
     tiles = [(i, j) for i in range(nb) for j in range(i + 1)]
-    keep = (
-        lax.broadcasted_iota(jnp.int32, (block, block), 0)
-        >= lax.broadcasted_iota(jnp.int32, (block, block), 1)
-    )
-
-    def decay_of(h, i, j):
-        col = cols[h, i * block : (i + 1) * block, :]
-        col = jnp.concatenate([col] * (block // dim), axis=1)
-        row = rows[pl.ds(h, 1), j * block : (j + 1) * block]
-        value = jnp.exp(jnp.minimum(col - row, 0.0))
-        return jnp.where(keep, value, 0.0) if i == j else value
+    sub = block // dim
 
     def span_of(i):
         return slice(i * block, (i + 1) * block)
 
-    def intra(h):
-        for i in range(nb):
-            total = None
-            for j in range(i + 1):
-                s = nt(q[span_of(i), lane(h)], k[span_of(j), lane(h)])
-                p = (s * decay_of(h, i, j)).astype(BF16)
-                probs[h, tiles.index((i, j))] = p
-                o = nn(p, v[span_of(j), lane(h)])
-                total = o if total is None else total + o
-            attn[span_of(i), lane(h)] = total
-
-    def both(body):
-        def pair(c):
-            body(mine(c))
-            body(others(c))
-
-        return pair
+    def decayed(s, h, i, j):
+        row = rows[pl.ds(h, 1), j * block : (j + 1) * block]
+
+        def parted(x, t, lo, hi):
+            m = cols[h, j * block + hi - 1 : j * block + hi, :]
+            width = (hi - lo) // dim
+            right = jnp.exp2(jnp.concatenate([m] * width, axis=1) - row[:, lo:hi])
+            left = jnp.exp2(cols[h, t : t + x.shape[0], :] - m)
+            return (x * right) * jnp.concatenate([left] * width, axis=1)
+
+        if i != j:
+            return parted(s, i * block, 0, block).astype(BF16)
+        lines = []
+        for a in range(sub):
+            t = slice(a * dim, (a + 1) * dim)
+            line = []
+            if a:
+                for b in range(a):
+                    line.append(
+                        parted(s[t, b * dim : (b + 1) * dim], i * block + a * dim, b * dim, (b + 1) * dim)
+                    )
+            gap = cols[h, i * block + a * dim : i * block + (a + 1) * dim, :] - row[:, t]
+            line.append(s[t, t] * jnp.exp2(gap + bias[...]))
+            if a + 1 < sub:
+                line.append(jnp.zeros((dim, (sub - 1 - a) * dim), F32))
+            lines.append(jnp.concatenate([x.astype(BF16) for x in line], axis=1))
+        return jnp.concatenate(lines, axis=0)
+
+    def before_norm(h, i):
+        r = span_of(i)
+        grow = jnp.exp2(cols[h, r, :])
+        grown[r, lane(h)] = (q[r, lane(h)].astype(F32) * grow).astype(BF16)
+        s = jax.nn.sigmoid(gate[r, lane(h)].astype(F32))
+        sig[h, r, :] = s
+        dnorm[h, r, :] = up[r, lane(h)].astype(F32) * s
+
+    def intra_pair(c):
+        work = [(h, i, j) for h in (mine(c), others(c)) for i, j in tiles]
+
+        def scores(h, i, j):
+            return nt(q[span_of(i), lane(h)], k[span_of(j), lane(h)])
+
+        ahead = scores(*work[0])
+        total = None
+        for n, (h, i, j) in enumerate(work):
+            s = ahead
+            if n + 1 < len(work):
+                ahead = scores(*work[n + 1])
+            p = decayed(s, h, i, j)
+            probs[h, tiles.index((i, j))] = p
+            o = nn(p, v[span_of(j), lane(h)])
+            total = o if j == 0 else total + o
+            if i == j:
+                inside[h, span_of(i), :] = total
+                before_norm(h, i)
 
     def finish_attn(c):
         put(0, c, state)
@@ -317,11 +360,10 @@
             r = span_of(i)
             square, inner = scale_ref[r, :], center_ref[r, :]
             for h in (mine(c), others(c)):
-                a = attn[r, lane(h)] + jnp.exp(cols[h, r, :]) * nn(q[r, lane(h)], state[h])
-                attn[r, lane(h)] = a
+                a = inside[h, r, :] + nn(grown[r, lane(h)], state[h])
+                attn[h, r, :] = a
                 square = square + a * a
-                sig = jax.nn.sigmoid(gate[r, lane(h)].astype(F32))
-                inner = inner + up[r, lane(h)].astype(F32) * sig * a
+                inner = inner + dnorm[h, r, :] * a
             scale_ref[r, :] = square
             center_ref[r, :] = inner
 
@@ -330,7 +372,7 @@
     loads[3].wait()
     loads[4].wait()
     loads[5].wait()
-    ticks(0, both(intra), 0, finish_attn)
+    ticks(0, intra_pair, 0, finish_attn)
 
     strips = tokens // 128
 
@@ -368,15 +410,13 @@
         for i in range(nb):
             r = span_of(i)
             sc = scale_ref[r, :]
-            normed = attn[r, lane(h)] * sc
-            sig = jax.nn.sigmoid(gate[r, lane(h)].astype(F32))
-            dnorm = up[r, lane(h)].astype(F32) * sig
-            g = (sc * (dnorm - normed * center_ref[r, :])).astype(BF16)
+            s, d = sig[h, r, :], dnorm[h, r, :]
+            normed = attn[h, r, :] * sc
+            g = (sc * (d - normed * center_ref[r, :])).astype(BF16)
             grad[r, lane(h)] = g
-            up[r, lane(h)] = (normed * sig).astype(BF16)
-            gate[r, lane(h)] = (dnorm * normed * (1.0 - sig)).astype(BF16)
-            grown = (q[r, lane(h)].astype(F32) * jnp.exp(cols[h, r, :])).astype(BF16)
-            w = tn(grown, g)
+            up[r, lane(h)] = (normed * s).astype(BF16)
+            gate[r, lane(h)] = (d * normed * (1.0 - s)).astype(BF16)
+            w = tn(grown[r, lane(h)], g)
             weighted = w if weighted is None else weighted + w
         own[1, h] = weighted
 
@@ -389,47 +429,60 @@
 
     first_exchange(1, pointwise_pair, 3)
 
-    def backward(h):
-        dq = [None] * nb
-        dk = [None] * nb
-        dv = [None] * nb
+    def backward_pair(c):
+        pair = (mine(c), others(c))
+        work = [(e, i, j) for e in (0, 1) for i, j in tiles]
+
+        def scores(e, i, j):
+            return nt(grad[span_of(i), lane(pair[e])], v[span_of(j), lane(pair[e])])
 
         def add(parts, n, x):
-            parts[n] = x if parts[n] is None else parts[n] + x
-
-        for i, j in tiles:
-            g = grad[span_of(i), lane(h)]
-            pg = (nt(g, v[span_of(j), lane(h)]) * decay_of(h, i, j)).astype(BF16)
-            add(dq, i, nn(pg, k[span_of(j), lane(h)]))
-            add(dk, j, tn(pg, q[span_of(i), lane(h)]))
-            add(dv, j, tn(probs[h, tiles.index((i, j))], g))
-        for i in range(nb):
+            parts[n] = x if n not in parts else parts[n] + x
+
+        ahead = scores(*work[0])
+        dq, dk, dv = {}, {}, {}
+        for n, (e, i, j) in enumerate(work):
+            h = pair[e]
+            s = ahead
+            if n + 1 < len(work):
+                ahead = scores(*work[n + 1])
             r = span_of(i)
-            carried = jnp.exp(cols[h, r, :]) * nt(grad[r, lane(h)], state[h])
-            q[r, lane(h)] = (dq[i] + carried).astype(BF16)
-            attn[r, lane(h)] = dk[i]
-            dvp[r, lane(h)] = dv[i]
-
-    ticks(1, both(backward), 1, lambda c: put(1, c, state_grad))
+            add(dv, (e, j), tn(grad[r, lane(h)], probs[h, tiles.index((i, j))]))
+            pg = decayed(s, h, i, j)
+            add(dk, (e, j), tn(q[r, lane(h)], pg))
+            add(dq, (e, i), nn(pg, k[span_of(j), lane(h)]))
+            if i == j:
+                carried = jnp.exp2(cols[h, r, :]) * nt(grad[r, lane(h)], state[h])
+                grown[r, lane(h)] = (dq[e, i] + carried).astype(BF16)
+            if i == nb - 1:
+                dkt[h, :, span_of(j)] = dk[e, j]
+                dvt[h, :, span_of(j)] = dv[e, j]
+
+    ticks(1, backward_pair, 1, lambda c: put(1, c, state_grad))
 
     for b in range(bits):
         sp_copy(b).wait_send()
     for d in (0, 1):
-
-        @pl.loop(0, heads)
-        def _(h):
-            s0_copy(d, h).wait_send()
-
-        @pl.loop(0, half)
-        def _(c):
-            for s in range(chips - 1):
-                st_copy(d, s, c).wait_send()
-
-            @pl.when(takes(d, chips) == 0)
-            def _():
-                st_copy(d, chips - 1, c).wait_send()
-
-            fin_copy(d, c).wait_send()
+        for b in (0, 1):
+            part = pl.ds(b * half, half)
+            pltpu.make_async_remote_copy(
+                src_ref=own.at[d, part], dst_ref=other.at[d, part], send_sem=s0_send.at[d],
+                recv_sem=s0_recv.at[d, 0], device_id=partner(0), device_id_type=MESH,
+            ).wait_send()
+
+        def all_sent(s):
+            pltpu.make_async_remote_copy(
+                src_ref=sent.at[d, s], dst_ref=got.at[d, s], send_sem=st_send.at[d, s],
+                recv_sem=st_recv.at[d, s, 0], device_id=partner(s + 1), device_id_type=MESH,
+            ).wait_send()
+
+        for s in range(chips - 1):
+            all_sent(s)
+        pl.when(takes(d, chips) == 0)(lambda: all_sent(chips - 1))
+        pltpu.make_async_remote_copy(
+            src_ref=edge.at[d], dst_ref=far.at[d], send_sem=fin_send.at[d],
+            recv_sem=fin_recv.at[d, 0], device_id=partner(0), device_id_type=MESH,
+        ).wait_send()
 
     for d in range(1, n_tp):
         tp_copy(d).wait_send()
@@ -437,7 +490,7 @@
 
 def last_kernel(
     heads, dim, tokens,
-    out_ref, gg_ref, dq_ref, k, v, dkp, dvp, state_grad, cols,
+    out_ref, gg_ref, dq_ref, k, v, dkt, dvt, state_grad, rows,
     out_hbm, dq_hbm, dk_hbm, dv_hbm, gg_hbm,
     dk, dv, sem, pair_sem,
 ):
@@ -453,7 +506,7 @@
     def strips(i):
         part = pl.ds(pl.multiple_of(i * 2 * dim, 2 * dim), 2 * dim)
         return [
-            pltpu.make_async_copy(a.at[:, part], b.at[:, part], pair_sem.at[n, i])
+            pltpu.make_async_copy(a.at[:, part], b.at[:, part], pair_sem.at[n])
             for n, (a, b) in enumerate(((dk, dk_hbm), (dv, dv_hbm)))
         ]
 
@@ -461,22 +514,20 @@
     def _(i):
         for h in (2 * i, 2 * i + 1):
             at = pl.ds(pl.multiple_of(h * dim, dim), dim)
-            last = cols[h, tokens - 1 : tokens, :]
+            row = rows[pl.ds(h, 1), :]
+            tail = jnp.exp2(row[:, tokens - 1 : tokens] - row)
+            turned = state_grad[h].astype(F32).T.astype(BF16)
             for n in range(tokens // block):
                 r = slice(n * block, (n + 1) * block)
-                tail = jnp.exp(last - cols[h, r, :])
-                key = dkp[r, at] + tail * nt(v[r, at], state_grad[h])
-                value = dvp[r, at] + tail * nn(k[r, at], state_grad[h])
-                dk[r, at] = key.astype(BF16)
-                dv[r, at] = value.astype(BF16)
+                key = dkt[h, :, r] + tail[:, r] * nt(state_grad[h], v[r, at])
+                value = dvt[h, :, r] + tail[:, r] * nt(turned, k[r, at])
+                dk[r, at] = key.astype(BF16).T
+                dv[r, at] = value.astype(BF16).T
         for c in strips(i):
             c.start()
 
-    @pl.loop(0, trips)
-    def _(i):
-        for c in strips(i):
-            c.wait()
-
+    for n, (a, b) in enumerate(((dk, dk_hbm), (dv, dv_hbm))):
+        pltpu.make_async_copy(a, b, pair_sem.at[n]).wait()
     for c in whole:
         c.wait()
 
@@ -500,19 +551,20 @@
         hbm = pl.BlockSpec(memory_space=pltpu.HBM)
         vmem = pl.BlockSpec(memory_space=pltpu.VMEM)
         big = pltpu.VMEM((tokens, flat), BF16)
-        wide = pltpu.VMEM((tokens, flat), F32)
+        wide = pltpu.VMEM((heads, tokens, dim), F32)
+        turned = pltpu.VMEM((heads, dim, tokens), F32)
         flops = 2 * tokens * tokens * flat * 5 + 2 * tokens * flat * dim * 7
-        up, gg, dq, k, v, dkp, dvp, state_grad, cols = pl.pallas_call(
+        results = pl.pallas_call(
             functools.partial(kernel, n_seq, n_tp, heads, dim, tokens),
             out_shape=[
-                big, big, big, big, big, wide, wide,
-                pltpu.VMEM((heads, *tile), BF16), pltpu.VMEM((heads, tokens, dim), F32),
+                big, big, big, big, big, turned, turned,
+                pltpu.VMEM((heads, *tile), BF16), pltpu.VMEM((heads, tokens), F32),
             ],
             in_specs=[hbm] * 6,
             out_specs=[vmem] * 9,
             scratch_shapes=[
-                pltpu.VMEM((heads, tokens), F32), pltpu.VMEM((heads, tokens), F32),
-                pltpu.VMEM((tokens, 128), BF16), big,
+                pltpu.VMEM((heads, tokens), F32), big, wide, pltpu.VMEM((tokens, 128), BF16),
+                pltpu.VMEM(tile, F32), wide, wide, wide, wide, big,
                 pltpu.VMEM((heads, nb * (nb + 1) // 2, block, block), BF16),
                 pltpu.VMEM((2, heads, *tile), F32),
                 pltpu.VMEM((2, heads, *tile), F32),
@@ -525,12 +577,12 @@
                 pltpu.VMEM((2, bits, 3, heads, dim), F32),
                 pltpu.VMEM(sums, F32), pltpu.VMEM((peers, *sums), F32),
                 pltpu.VMEM((tokens, dim), F32), pltpu.VMEM((tokens, dim), F32),
-                dma((6,)), dma((bits,)), dma((bits,)), dma((2, heads)), dma((2, heads)),
-                dma((2, chips, half)), dma((2, chips, half)), dma((2, half)), dma((2, half)),
+                dma((6,)), dma((bits,)), dma((bits,)), dma((2,)), dma((2, heads)),
+                dma((2, chips)), dma((2, chips, half)), dma((2,)), dma((2, half)),
                 dma((peers,)), dma((peers,)),
             ],
             compiler_params=pltpu.CompilerParams(
-                collective_id=0, has_side_effects=True, vmem_limit_bytes=36 << 20
+                collective_id=0, has_side_effects=True, vmem_limit_bytes=43 << 20
             ),
             cost_estimate=pl.CostEstimate(
                 flops=flops, bytes_accessed=tokens * flat * 10, transcendentals=0
@@ -542,12 +594,12 @@
                 out_shape=[jax.ShapeDtypeStruct((tokens, flat), BF16)] * 5,
                 in_specs=[vmem] * 9,
                 out_specs=[hbm] * 5,
-                scratch_shapes=[big, big, dma((3,)), dma((2, half))],
+                scratch_shapes=[big, big, dma((3,)), dma((2,))],
                 compiler_params=pltpu.CompilerParams(vmem_limit_bytes=16 << 20),
                 cost_estimate=pl.CostEstimate(
                     flops=4 * tokens * flat * dim, bytes_accessed=tokens * flat * 10, transcendentals=0
                 ),
-            )(up, gg, dq, k, v, dkp, dvp, state_grad, cols)
+            )(*results)
         )
 
     spec = P("seq", "tp")

time: 66 us -> 59.4 us (0.900)
  Pallas kernels: 65 us -> 58.6 us
    pallas_call x1, Pallas kernels: 60.9 us -> 54.4 us  [shards(): pl.pallas_call(functools.partial(kernel, n_seq, n_tp, heads, dim, tokens)...]
where the time goes in v2:
time: 59.4 us; the launch traced here: 59.3 us
  Pallas kernels  58.6 us (99%)
  between operations  0.64 us (1%)
    pallas_call x1, Pallas kernels, shards(): pl.pallas_call(functools.partial(kernel, n_seq, n_tp, heads, dim, tokens)...  54.4 us
    pallas_call x1, Pallas kernels, shards(): pl.pallas_call(functools.partial(last_kernel, heads, dim, tokens), out_sh...  4.18 us

profile of v2, /device:TPU:0, one launch (start us, length us, event | category | flops | bytes accessed | tf_op | source)
XLA Modules:
  0.0 59.3 jit_solution(18368186401813955779)
XLA Ops:
  0.6 54.4 %shard_map.101 = (bf16[512,2048]{1,0:T(8,128)(2,1)S(1)}, bf16[512,2048]{1,0:T(8,128)(2,1)S(1)}, bf16[512,2048]{1,0:T(8,128)(2,1)S(1)}, bf16[512,2048]{1,0:T(8,12...) custom-call(bf16[512,2048]{1,0:T(8,128)(2,1)} %q_hbm.1, ...), custom_call_target="tpu_custom_call" | custom-call | flops 7247757312 | bytes 10485760 | tf_op jit(solution)/shard_map/pallas_call | solution.py:557
  55.1 4.2 %shard_map.102 = (bf16[512,2048]{1,0:T(8,128)(2,1)}, bf16[512,2048]{1,0:T(8,128)(2,1)}, bf16[512,2048]{1,0:T(8,128)(2,1)}, bf16[512,2048]{1,0:T(8,128)(2,1)}, bf16[512,2048]{1,0:T(8,128)(2,1)}) custom-call(bf16[512,2048]{1,0:T(8,128)(2,1)S(1)} %get-tuple-element.14.out_ref, bf16[512,2048]{1,0:T(8,128)(2,1)S(1)} %get-tuple-element.15.gg_ref, ...), custom_call_target="tpu_custom_call" | custom-call | flops 536870912 | bytes 10485760 | tf_op jit(solution)/shard_map/pallas_call | solution.py:592

commit v3 on v2

--- a/solution.py
+++ b/solution.py
@@ -71,13 +71,24 @@
     def load(i, a, b):
         return pltpu.make_async_copy(a, b, in_sem.at[i])
 
-    loads = [
-        load(i, a, b)
-        for i, (a, b) in enumerate(
-            ((rate_hbm, rate), (k_hbm, k), (v_hbm, v), (q_hbm, q), (up_hbm, up), (gate_hbm, gate))
-        )
-    ]
-    for c in loads[:3]:
+    rate_load = load(0, rate_hbm, rate)
+    q_load, up_load, gate_load = (
+        load(1 + i, a, b) for i, (a, b) in enumerate(((q_hbm, q), (up_hbm, up), (gate_hbm, gate)))
+    )
+    soon = min(2, half)
+
+    def kv_loads(lo, hi, at):
+        out = []
+        for start in (lo, half + lo):
+            part = slice(start * dim, (start + hi - lo) * dim)
+            for a, b in ((k_hbm, k), (v_hbm, v)):
+                out.append(load(4 + at + len(out), a.at[:, part], b.at[:, part]))
+        return out
+
+    first_loads = kv_loads(0, soon, 0)
+    more_loads = kv_loads(soon, half, 4) if soon < half else []
+    rate_load.start()
+    for c in first_loads + more_loads:
         c.start()
 
     barrier = pltpu.get_barrier_semaphore()
@@ -97,7 +108,7 @@
     def others(c):
         return (1 - core) * half + c
 
-    loads[0].wait()
+    rate_load.wait()
     upto = (
         lax.broadcasted_iota(jnp.int32, (tokens, tokens), 0)
         <= lax.broadcasted_iota(jnp.int32, (tokens, tokens), 1)
@@ -108,15 +119,14 @@
     rows[...] = across
     split[...] = stacked(across).T.astype(BF16)
     span[0] = jnp.broadcast_to(across[:, tokens - 1 : tokens], (heads, dim))
-    loads[3].start()
+    q_load.start()
     corner = lax.broadcasted_iota(jnp.int32, (dim, dim), 0) >= lax.broadcasted_iota(
         jnp.int32, (dim, dim), 1
     )
     bias[...] = jnp.where(corner, 0.0, LOW)
 
-    @pl.loop(0, half)
-    def _(i):
-        pair = (2 * i, 2 * i + 1)
+    def cols_pair(c):
+        pair = (mine(c), others(c))
         at = lax.broadcasted_iota(jnp.int32, (128, dim), 0)
         pick = jnp.concatenate(
             [
@@ -130,7 +140,7 @@
             for n, h in enumerate(pair):
                 cols[h, r, :] = wide[:, n * dim : (n + 1) * dim]
 
-    pl.semaphore_wait(barrier, bits + n_tp - 1)
+    crossed = chips == 2 and half % 2 == 0
 
     def sp_copy(b):
         return pltpu.make_async_remote_copy(
@@ -138,7 +148,11 @@
             recv_sem=sp_recv.at[b], device_id=partner(b), device_id_type=MESH,
         )
 
-    sp_copy(0).start()
+    def aside_copy():
+        return pltpu.make_async_remote_copy(
+            src_ref=span_in.at[1], dst_ref=span_in.at[bits], send_sem=sp_send.at[bits],
+            recv_sem=sp_recv.at[bits], device_id=partner(2), device_id_type=MESH,
+        )
 
     def s0_copy(d, h):
         return pltpu.make_async_remote_copy(
@@ -164,6 +178,15 @@
         if b + 1 < bits:
             span[b + 1] = here + there
             sp_copy(b + 1).start()
+        if crossed and b == 1:
+            aside_copy().start()
+        if crossed and b == 2:
+            aside_copy().wait_recv()
+            aside = span_in[bits]
+            for d in (0, 1):
+                f = takes(d, 1).astype(F32)
+                factor[d, bits, 0] = jnp.exp2(aside + span[1])
+                factor[d, bits, 1] = jnp.exp2(f * span_in[1] + (1.0 - f) * aside)
         for d in (0, 1):
             f = takes(d, b).astype(F32)
             factor[d, b, 0] = jnp.exp2(there * (1.0 - f))
@@ -188,11 +211,96 @@
         else:
             st_copy(d, s, c).start()
 
-    def level0(d, c):
+    def level0(d, c, crosses):
         h = mine(c)
         s0_copy(d, h).wait_recv()
-        sent[d, 0, c] = row_of(d, 0, 0, h) * own[d, h] + row_of(d, 0, 1, h) * other[d, h]
-        send_level(d, 0, c)
+        total = row_of(d, 0, 0, h) * own[d, h] + row_of(d, 0, 1, h) * other[d, h]
+        if not crossed:
+            sent[d, 0, c] = total
+            send_level(d, 0, c)
+        elif crosses:
+            sent[d, 1, c] = total
+
+            @pl.when(takes(d, 2) == 0)
+            def _():
+                st_copy(d, 1, c).start()
+        else:
+            sent[d, 0, c] = total
+
+            @pl.when((takes(d, 1) == 0) | (takes(d, 2) == 0))
+            def _():
+                st_copy(d, 0, c).start()
+
+    def even_first(d, c):
+        h = mine(c)
+        fx, fy = takes(d, 1), takes(d, 2)
+
+        @pl.when((fx == 1) | (fy == 0))
+        def _():
+            st_copy(d, 0, c).wait_recv()
+            theirs = got[d, 0, c]
+            edge[d, c] = fx.astype(F32) * theirs
+
+            @pl.when(fy == 0)
+            def _():
+                sent[d, 1, c] = row_of(d, 1, 0, h) * sent[d, 0, c] + row_of(d, 1, 1, h) * theirs
+                st_copy(d, 1, c).start()
+
+        @pl.when((fx == 0) & (fy == 1))
+        def _():
+            edge[d, c] = jnp.zeros((dim, dim), F32)
+
+    def even_second(d, c):
+        @pl.when(takes(d, 2) == 1)
+        def _():
+            st_copy(d, 1, c).wait_recv()
+            edge[d, c] = edge[d, c] + row_of(d, 2, 2, mine(c)) * got[d, 1, c]
+
+        fin_copy(d, c).start()
+
+    def odd_first(d, c):
+        fx, fy = takes(d, 1), takes(d, 2)
+
+        @pl.when(fy == 1)
+        def _():
+            st_copy(d, 1, c).wait_recv()
+
+        @pl.when((fx == 0) & (fy == 1))
+        def _():
+            sent[d, 0, c] = row_of(d, bits, 0, mine(c)) * got[d, 1, c] + sent[d, 1, c]
+
+        @pl.when((fx == 1) & (fy == 1))
+        def _():
+            sent[d, 0, c] = got[d, 1, c]
+
+        @pl.when((fx == 0) & (fy == 0))
+        def _():
+            sent[d, 0, c] = sent[d, 1, c]
+
+        @pl.when((fx == 0) | (fy == 1))
+        def _():
+            st_copy(d, 0, c).start()
+
+    def odd_second(d, c):
+        fx, fy = takes(d, 1), takes(d, 2)
+
+        @pl.when((fx == 1) | (fy == 1))
+        def _():
+            st_copy(d, 0, c).wait_recv()
+
+        @pl.when(fy == 1)
+        def _():
+            edge[d, c] = got[d, 0, c] + row_of(d, bits, 1, mine(c)) * got[d, 1, c]
+
+        @pl.when((fx == 1) & (fy == 0))
+        def _():
+            edge[d, c] = got[d, 0, c]
+
+        @pl.when((fx == 0) & (fy == 0))
+        def _():
+            edge[d, c] = jnp.zeros((dim, dim), F32)
+
+        fin_copy(d, c).start()
 
     def step(d, s, c):
         h = mine(c)
@@ -237,60 +345,102 @@
             scaled.append((k[:, lane(h)].astype(F32) * jnp.exp2(last - cols[h])).astype(BF16))
         for h, x in zip(pair, scaled):
             own[0, h] = tn(x, v[:, lane(h)])
-        for h in pair:
-            s0_copy(0, h).start()
-
-    def first_exchange(d, body, lead):
-        lead = min(lead, half)
-
-        @pl.loop(0, lead)
+
+    def local_and_next(c):
+        local_pair(c)
+        cols_pair(c + 1 - (c + 1) // half)
+
+    def s0_start(d, c):
+        for h in (others(c), mine(c)):
+            s0_copy(d, h).start()
+
+    def levels0(d, lo, hi, lag, body):
+        count = 2 if crossed else 1
+
+        @pl.loop(0, (hi - lo) // count)
+        def _(n):
+            for e in range(count):
+                c = lo + n * count + e
+                body(c)
+                level0(d, c - lag, (e + lo - lag) % 2 == 1)
+
+    def first_exchange(d, body, done):
+        lead = min(2, half)
+
+        @pl.loop(done, lead)
         def _(c):
             body(c)
+            s0_start(d, c)
 
         if d == 0:
             span_step(0)
 
-        @pl.loop(lead, half)
-        def _(c):
+        def more(c):
             body(c)
-            level0(d, c - lead)
-
+            s0_start(d, c)
+
+        levels0(d, lead, half, lead, more)
         if d == 0:
-            for b in range(1, bits):
-                span_step(b)
-
-        @pl.loop(half - lead, half)
-        def _(c):
-            level0(d, c)
-
-    def ticks(d, body, early, finish):
-        lags = [2 * s - early for s in range(chips)]
-        lag = lags[-1] + 1
-        for s in range(chips):
-            for c in range(max(0, -lags[s])):
-                step(d, s, c)
-
-        @pl.loop(0, half + lag)
+            span_step(1)
+        levels0(d, half, half + lead, lead, lambda c: None)
+
+    def ticks(d, body, finish):
+        if crossed:
+            trips = half // 2
+
+            def first(m):
+                even_first(d, 2 * m)
+                odd_first(d, 2 * m + 1)
+
+            def second(m):
+                even_second(d, 2 * m)
+                odd_second(d, 2 * m + 1)
+
+            def third(m):
+                finish(2 * m)
+                finish(2 * m + 1)
+
+            stages = [(0, first), (trips, second), (trips + 1, third)]
+        else:
+            trips = half
+            stages = [(2 * s, functools.partial(step, d, s)) for s in range(chips)]
+            stages.append((2 * chips - 1, finish))
+
+        @pl.loop(0, max(half, trips + stages[-1][0]))
         def _(t):
             @pl.when(t < half)
             def _():
                 body(t)
 
-            for s in range(chips):
-
-                @pl.when((t >= max(0, lags[s])) & (t < half + lags[s]))
+            for n, (lag, stage) in enumerate(stages):
+                if d == 0 and 1 <= n + 1 < bits and n >= 1 and not crossed:
+
+                    @pl.when(t == lag)
+                    def _():
+                        span_step(n + 1)
+
+                if d == 0 and crossed and n == 0:
+
+                    @pl.when(t == 0)
+                    def _():
+                        span_step(2)
+
+                @pl.when((t >= lag) & (t < trips + lag))
                 def _():
-                    step(d, s, t - lags[s])
-
-            @pl.when(t >= lag)
-            def _():
-                finish(t - lag)
-
-    loads[1].wait()
-    loads[2].wait()
-    first_exchange(0, local_pair, 3)
-    loads[4].start()
-    loads[5].start()
+                    stage(t - lag)
+
+    cols_pair(0)
+    for c in first_loads:
+        c.wait()
+    local_and_next(0)
+    pl.semaphore_wait(barrier, bits + n_tp - 1)
+    sp_copy(0).start()
+    s0_start(0, 0)
+    for c in more_loads:
+        c.wait()
+    up_load.start()
+    gate_load.start()
+    first_exchange(0, local_and_next, 1)
 
     tiles = [(i, j) for i in range(nb) for j in range(i + 1)]
     sub = block // dim
@@ -369,10 +519,10 @@
 
     scale_ref[...] = jnp.zeros_like(scale_ref)
     center_ref[...] = jnp.zeros_like(center_ref)
-    loads[3].wait()
-    loads[4].wait()
-    loads[5].wait()
-    ticks(0, intra_pair, 0, finish_attn)
+    q_load.wait()
+    up_load.wait()
+    gate_load.wait()
+    ticks(0, intra_pair, finish_attn)
 
     strips = tokens // 128
 
@@ -424,10 +574,8 @@
         pair = (others(c), mine(c))
         for h in pair:
             pointwise(h)
-        for h in pair:
-            s0_copy(1, h).start()
-
-    first_exchange(1, pointwise_pair, 3)
+
+    first_exchange(1, pointwise_pair, 0)
 
     def backward_pair(c):
         pair = (mine(c), others(c))
@@ -458,10 +606,12 @@
                 dkt[h, :, span_of(j)] = dk[e, j]
                 dvt[h, :, span_of(j)] = dv[e, j]
 
-    ticks(1, backward_pair, 1, lambda c: put(1, c, state_grad))
+    ticks(1, backward_pair, lambda c: put(1, c, state_grad))
 
     for b in range(bits):
         sp_copy(b).wait_send()
+    if crossed:
+        aside_copy().wait_send()
     for d in (0, 1):
         for b in (0, 1):
             part = pl.ds(b * half, half)
@@ -470,15 +620,20 @@
                 recv_sem=s0_recv.at[d, 0], device_id=partner(0), device_id_type=MESH,
             ).wait_send()
 
-        def all_sent(s):
+        def sent_all(s, count):
+            part = pl.ds(0, count)
             pltpu.make_async_remote_copy(
-                src_ref=sent.at[d, s], dst_ref=got.at[d, s], send_sem=st_send.at[d, s],
+                src_ref=sent.at[d, s, part], dst_ref=got.at[d, s, part], send_sem=st_send.at[d, s],
                 recv_sem=st_recv.at[d, s, 0], device_id=partner(s + 1), device_id_type=MESH,
             ).wait_send()
 
-        for s in range(chips - 1):
-            all_sent(s)
-        pl.when(takes(d, chips) == 0)(lambda: all_sent(chips - 1))
+        if crossed:
+            pl.when(takes(d, 1) == 0)(lambda: sent_all(0, half))
+            pl.when(takes(d, 1) == 1)(lambda: sent_all(0, half // 2))
+        else:
+            for s in range(chips - 1):
+                sent_all(s, half)
+        pl.when(takes(d, chips) == 0)(lambda: sent_all(chips - 1, half))
         pltpu.make_async_remote_copy(
             src_ref=edge.at[d], dst_ref=far.at[d], send_sem=fin_send.at[d],
             recv_sem=fin_recv.at[d, 0], device_id=partner(0), device_id_type=MESH,
@@ -573,11 +728,11 @@
                 pltpu.VMEM((2, half, *tile), F32),
                 pltpu.VMEM((2, half, *tile), F32),
                 pltpu.VMEM((heads, *tile), BF16),
-                pltpu.VMEM((bits, heads, dim), F32), pltpu.VMEM((bits, heads, dim), F32),
-                pltpu.VMEM((2, bits, 3, heads, dim), F32),
+                pltpu.VMEM((bits, heads, dim), F32), pltpu.VMEM((bits + 1, heads, dim), F32),
+                pltpu.VMEM((2, bits + 1, 3, heads, dim), F32),
                 pltpu.VMEM(sums, F32), pltpu.VMEM((peers, *sums), F32),
                 pltpu.VMEM((tokens, dim), F32), pltpu.VMEM((tokens, dim), F32),
-                dma((6,)), dma((bits,)), dma((bits,)), dma((2,)), dma((2, heads)),
+                dma((12,)), dma((bits + 1,)), dma((bits + 1,)), dma((2,)), dma((2, heads)),
                 dma((2, chips)), dma((2, chips, half)), dma((2,)), dma((2, half)),
                 dma((peers,)), dma((peers,)),
             ],

time: 59.4 us -> 50.6 us (0.85)
  Pallas kernels: 58.6 us -> 49.8 us
    pallas_call x1, Pallas kernels: 54.4 us -> 45.7 us  [shards(): pl.pallas_call(functools.partial(kernel, n_seq, n_tp, heads, dim, tokens)...]
where the time goes in v3:
time: 50.6 us; the launch traced here: 50.5 us
  Pallas kernels  49.8 us (98%)
  between operations  0.64 us (1%)
    pallas_call x1, Pallas kernels, shards(): pl.pallas_call(functools.partial(kernel, n_seq, n_tp, heads, dim, tokens)...  45.7 us
    pallas_call x1, Pallas kernels, shards(): pl.pallas_call(functools.partial(last_kernel, heads, dim, tokens), out_sh...  4.18 us

profile of v3, /device:TPU:0, one launch (start us, length us, event | category | flops | bytes accessed | tf_op | source)
XLA Modules:
  0.0 50.5 jit_solution(1671819084371534866)
XLA Ops:
  0.6 45.7 %shard_map.101 = (bf16[512,2048]{1,0:T(8,128)(2,1)S(1)}, bf16[512,2048]{1,0:T(8,128)(2,1)S(1)}, bf16[512,2048]{1,0:T(8,128)(2,1)S(1)}, bf16[512,2048]{1,0:T(8,12...) custom-call(bf16[512,2048]{1,0:T(8,128)(2,1)} %q_hbm.1, ...), custom_call_target="tpu_custom_call" | custom-call | flops 7247757312 | bytes 10485760 | tf_op jit(solution)/shard_map/pallas_call | solution.py:712
  46.3 4.2 %shard_map.102 = (bf16[512,2048]{1,0:T(8,128)(2,1)}, bf16[512,2048]{1,0:T(8,128)(2,1)}, bf16[512,2048]{1,0:T(8,128)(2,1)}, bf16[512,2048]{1,0:T(8,128)(2,1)}, bf16[512,2048]{1,0:T(8,128)(2,1)}) custom-call(bf16[512,2048]{1,0:T(8,128)(2,1)S(1)} %get-tuple-element.14.out_ref, bf16[512,2048]{1,0:T(8,128)(2,1)S(1)} %get-tuple-element.15.gg_ref, ...), custom_call_target="tpu_custom_call" | custom-call | flops 536870912 | bytes 10485760 | tf_op jit(solution)/shard_map/pallas_call | solution.py:747

commit v4 on v3

--- a/solution.py
+++ b/solution.py
@@ -24,6 +24,10 @@
 
 def nn(a, b):
     return lax.dot_general(a, b, (((1,), (0,)), ((), ())), preferred_element_type=F32)
+
+
+def t0(a, b):
+    return lax.dot_general(a, b, (((0,), (1,)), ((), ())), preferred_element_type=F32)
 
 
 def three_parts(x):
@@ -91,9 +95,14 @@
     for c in first_loads + more_loads:
         c.start()
 
+    crossed = chips == 2 and half % 2 == 0
     barrier = pltpu.get_barrier_semaphore()
-    for b in range(bits):
-        pl.semaphore_signal(barrier, inc=1, device_id=partner(b), device_id_type=MESH)
+    if crossed:
+        others_along = [(lax.rem(me + o, n_seq), z) for o in range(1, n_seq)]
+    else:
+        others_along = [partner(b) for b in range(bits)]
+    for at in others_along:
+        pl.semaphore_signal(barrier, inc=1, device_id=at, device_id_type=MESH)
     for d in range(1, n_tp):
         pl.semaphore_signal(
             barrier, inc=1, device_id=(me, lax.rem(z + d, n_tp)), device_id_type=MESH
@@ -140,18 +149,16 @@
             for n, h in enumerate(pair):
                 cols[h, r, :] = wide[:, n * dim : (n + 1) * dim]
 
-    crossed = chips == 2 and half % 2 == 0
-
     def sp_copy(b):
         return pltpu.make_async_remote_copy(
             src_ref=span.at[b], dst_ref=span_in.at[b], send_sem=sp_send.at[b],
             recv_sem=sp_recv.at[b], device_id=partner(b), device_id_type=MESH,
         )
 
-    def aside_copy():
+    def last_copy(o):
         return pltpu.make_async_remote_copy(
-            src_ref=span_in.at[1], dst_ref=span_in.at[bits], send_sem=sp_send.at[bits],
-            recv_sem=sp_recv.at[bits], device_id=partner(2), device_id_type=MESH,
+            src_ref=span.at[0], dst_ref=span_in.at[me], send_sem=sp_send.at[o],
+            recv_sem=sp_recv.at[o], device_id=(lax.rem(me + o, n_seq), z), device_id_type=MESH,
         )
 
     def s0_copy(d, h):
@@ -172,32 +179,59 @@
             recv_sem=fin_recv.at[d, c], device_id=partner(0), device_id_type=MESH,
         )
 
+    def set_factors(b, here, there, before):
+        for d in (0, 1):
+            f = takes(d, b).astype(F32)
+            factor[d, b, 0] = jnp.exp2(there * (1.0 - f))
+            factor[d, b, 1] = jnp.exp2(here * f)
+            factor[d, b, 2] = jnp.exp2(there * f) if b == 0 else f * jnp.exp2(before(d))
+
     def span_step(b):
+        if crossed:
+            return crossed_spans(b)
         sp_copy(b).wait_recv()
         here, there = span[b], span_in[b]
         if b + 1 < bits:
             span[b + 1] = here + there
             sp_copy(b + 1).start()
-        if crossed and b == 1:
-            aside_copy().start()
-        if crossed and b == 2:
-            aside_copy().wait_recv()
-            aside = span_in[bits]
-            for d in (0, 1):
-                f = takes(d, 1).astype(F32)
-                factor[d, bits, 0] = jnp.exp2(aside + span[1])
-                factor[d, bits, 1] = jnp.exp2(f * span_in[1] + (1.0 - f) * aside)
+
+        def before(d):
+            total = jnp.zeros((heads, dim), F32)
+            for r in range(1, b):
+                total = total + takes(d, r).astype(F32) * span_in[r]
+            return total
+
+        set_factors(b, here, there, before)
+
+    def crossed_spans(b):
+        if b == 0:
+            o = 1 + (1 - core) * (n_seq - 2)
+            last_copy(o).wait_recv()
+            set_factors(0, span[0], span_in[partner(0)[0]], None)
+            return
+        for o in range(1, n_seq):
+            if o == 1:
+                pl.when(core == 0)(lambda: last_copy(1).wait_recv())
+            elif o == n_seq - 1:
+                pl.when(core == 1)(lambda: last_copy(n_seq - 1).wait_recv())
+            else:
+                last_copy(o).wait_recv()
+
+        def chip(at):
+            first = at - lax.rem(at, 2)
+            return span_in[first] + span_in[first + 1]
+
+        span_in[me] = span[0]
+        mine_all, along_x, along_y = chip(me), chip(partner(1)[0]), chip(partner(2)[0])
+        aside = chip(partner(1)[0] + partner(2)[0] - me)
+        set_factors(1, mine_all, along_x, lambda d: jnp.zeros((heads, dim), F32))
+        set_factors(
+            2, mine_all + along_x, along_y + aside, lambda d: takes(d, 1).astype(F32) * along_x
+        )
         for d in (0, 1):
-            f = takes(d, b).astype(F32)
-            factor[d, b, 0] = jnp.exp2(there * (1.0 - f))
-            factor[d, b, 1] = jnp.exp2(here * f)
-            if b == 0:
-                factor[d, b, 2] = jnp.exp2(there * f)
-            else:
-                before = jnp.zeros((heads, dim), F32)
-                for r in range(1, b):
-                    before = before + takes(d, r).astype(F32) * span_in[r]
-                factor[d, b, 2] = f * jnp.exp2(before)
+            f = takes(d, 1).astype(F32)
+            factor[d, bits, 0] = jnp.exp2(aside + mine_all)
+            factor[d, bits, 1] = jnp.exp2(f * along_x + (1.0 - f) * aside)
 
     def row_of(d, b, n, h):
         return factor[d, b, n, pl.ds(h, 1), :]
@@ -380,9 +414,9 @@
             s0_start(d, c)
 
         levels0(d, lead, half, lead, more)
+        levels0(d, half, half + lead, lead, lambda c: None)
         if d == 0:
             span_step(1)
-        levels0(d, half, half + lead, lead, lambda c: None)
 
     def ticks(d, body, finish):
         if crossed:
@@ -419,12 +453,6 @@
                     def _():
                         span_step(n + 1)
 
-                if d == 0 and crossed and n == 0:
-
-                    @pl.when(t == 0)
-                    def _():
-                        span_step(2)
-
                 @pl.when((t >= lag) & (t < trips + lag))
                 def _():
                     stage(t - lag)
@@ -433,8 +461,12 @@
     for c in first_loads:
         c.wait()
     local_and_next(0)
-    pl.semaphore_wait(barrier, bits + n_tp - 1)
-    sp_copy(0).start()
+    pl.semaphore_wait(barrier, len(others_along) + n_tp - 1)
+    if crossed:
+        for o in range(1, n_seq):
+            last_copy(o).start()
+    else:
+        sp_copy(0).start()
     s0_start(0, 0)
     for c in more_loads:
         c.wait()
@@ -608,10 +640,12 @@
 
     ticks(1, backward_pair, lambda c: put(1, c, state_grad))
 
-    for b in range(bits):
-        sp_copy(b).wait_send()
     if crossed:
-        aside_copy().wait_send()
+        for o in range(1, n_seq):
+            last_copy(o).wait_send()
+    else:
+        for b in range(bits):
+            sp_copy(b).wait_send()
     for d in (0, 1):
         for b in (0, 1):
             part = pl.ds(b * half, half)
@@ -650,7 +684,8 @@
     dk, dv, sem, pair_sem,
 ):
     block = min(256, tokens)
-    trips = heads // 2
+    many = 4 if heads % 4 == 0 else 2
+    trips = heads // many
     whole = [
         pltpu.make_async_copy(a, b, sem.at[i])
         for i, (a, b) in enumerate(((out_ref, out_hbm), (gg_ref, gg_hbm), (dq_ref, dq_hbm)))
@@ -659,7 +694,7 @@
         c.start()
 
     def strips(i):
-        part = pl.ds(pl.multiple_of(i * 2 * dim, 2 * dim), 2 * dim)
+        part = pl.ds(pl.multiple_of(i * many * dim, many * dim), many * dim)
         return [
             pltpu.make_async_copy(a.at[:, part], b.at[:, part], pair_sem.at[n])
             for n, (a, b) in enumerate(((dk, dk_hbm), (dv, dv_hbm)))
@@ -667,15 +702,14 @@
 
     @pl.loop(0, trips)
     def _(i):
-        for h in (2 * i, 2 * i + 1):
+        for h in [many * i + n for n in range(many)]:
             at = pl.ds(pl.multiple_of(h * dim, dim), dim)
             row = rows[pl.ds(h, 1), :]
             tail = jnp.exp2(row[:, tokens - 1 : tokens] - row)
-            turned = state_grad[h].astype(F32).T.astype(BF16)
             for n in range(tokens // block):
                 r = slice(n * block, (n + 1) * block)
                 key = dkt[h, :, r] + tail[:, r] * nt(state_grad[h], v[r, at])
-                value = dvt[h, :, r] + tail[:, r] * nt(turned, k[r, at])
+                value = dvt[h, :, r] + tail[:, r] * t0(state_grad[h], k[r, at])
                 dk[r, at] = key.astype(BF16).T
                 dv[r, at] = value.astype(BF16).T
         for c in strips(i):
@@ -702,6 +736,7 @@
         tile = (dim, dim)
         dma = pltpu.SemaphoreType.DMA
         peers = max(n_tp - 1, 1)
+        spans = n_seq if chips == 2 else bits
         sums = (-(-2 * (tokens // 128) // 8) * 8, 128)
         hbm = pl.BlockSpec(memory_space=pltpu.HBM)
         vmem = pl.BlockSpec(memory_space=pltpu.VMEM)
@@ -728,11 +763,11 @@
                 pltpu.VMEM((2, half, *tile), F32),
                 pltpu.VMEM((2, half, *tile), F32),
                 pltpu.VMEM((heads, *tile), BF16),
-                pltpu.VMEM((bits, heads, dim), F32), pltpu.VMEM((bits + 1, heads, dim), F32),
+                pltpu.VMEM((bits, heads, dim), F32), pltpu.VMEM((n_seq, heads, dim), F32),
                 pltpu.VMEM((2, bits + 1, 3, heads, dim), F32),
                 pltpu.VMEM(sums, F32), pltpu.VMEM((peers, *sums), F32),
                 pltpu.VMEM((tokens, dim), F32), pltpu.VMEM((tokens, dim), F32),
-                dma((12,)), dma((bits + 1,)), dma((bits + 1,)), dma((2,)), dma((2, heads)),
+                dma((12,)), dma((spans,)), dma((spans,)), dma((2,)), dma((2, heads)),
                 dma((2, chips)), dma((2, chips, half)), dma((2,)), dma((2, half)),
                 dma((peers,)), dma((peers,)),
             ],

time: 50.6 us -> 49.1 us (0.970)
  Pallas kernels: 49.8 us -> 48.3 us
    pallas_call x1, Pallas kernels: 45.7 us -> 44.3 us  [shards(): pl.pallas_call(functools.partial(kernel, n_seq, n_tp, heads, dim, tokens)...]
where the time goes in v4:
time: 49.1 us; the launch traced here: 48.9 us
  Pallas kernels  48.3 us (98%)
  between operations  0.64 us (1%)
    pallas_call x1, Pallas kernels, shards(): pl.pallas_call(functools.partial(kernel, n_seq, n_tp, heads, dim, tokens)...  44.3 us
    pallas_call x1, Pallas kernels, shards(): pl.pallas_call(functools.partial(last_kernel, heads, dim, tokens), out_sh...  3.96 us

profile of v4, /device:TPU:0, one launch (start us, length us, event | category | flops | bytes accessed | tf_op | source)
XLA Modules:
  0.0 48.9 jit_solution(14491345526819942805)
XLA Ops:
  0.6 44.3 %shard_map.101 = (bf16[512,2048]{1,0:T(8,128)(2,1)S(1)}, bf16[512,2048]{1,0:T(8,128)(2,1)S(1)}, bf16[512,2048]{1,0:T(8,128)(2,1)S(1)}, bf16[512,2048]{1,0:T(8,12...) custom-call(bf16[512,2048]{1,0:T(8,128)(2,1)} %q_hbm.1, ...), custom_call_target="tpu_custom_call" | custom-call | flops 7247757312 | bytes 10485760 | tf_op jit(solution)/shard_map/pallas_call | solution.py:747
  45.0 4.0 %shard_map.102 = (bf16[512,2048]{1,0:T(8,128)(2,1)}, bf16[512,2048]{1,0:T(8,128)(2,1)}, bf16[512,2048]{1,0:T(8,128)(2,1)}, bf16[512,2048]{1,0:T(8,128)(2,1)}, bf16[512,2048]{1,0:T(8,128)(2,1)}) custom-call(bf16[512,2048]{1,0:T(8,128)(2,1)S(1)} %get-tuple-element.14.out_ref, bf16[512,2048]{1,0:T(8,128)(2,1)S(1)} %get-tuple-element.15.gg_ref, ...), custom_call_target="tpu_custom_call" | custom-call | flops 536870912 | bytes 10485760 | tf_op jit(solution)/shard_map/pallas_call | solution.py:782

commit v5 on v4

--- a/solution.py
+++ b/solution.py
@@ -431,8 +431,7 @@
                 odd_second(d, 2 * m + 1)
 
             def third(m):
-                finish(2 * m)
-                finish(2 * m + 1)
+                finish(2 * m, 2 * m + 1)
 
             stages = [(0, first), (trips, second), (trips + 1, third)]
         else:
@@ -510,8 +509,6 @@
 
     def before_norm(h, i):
         r = span_of(i)
-        grow = jnp.exp2(cols[h, r, :])
-        grown[r, lane(h)] = (q[r, lane(h)].astype(F32) * grow).astype(BF16)
         s = jax.nn.sigmoid(gate[r, lane(h)].astype(F32))
         sig[h, r, :] = s
         dnorm[h, r, :] = up[r, lane(h)].astype(F32) * s
@@ -536,13 +533,13 @@
                 inside[h, span_of(i), :] = total
                 before_norm(h, i)
 
-    def finish_attn(c):
-        put(0, c, state)
-        for i in range(nb):
-            r = span_of(i)
+    def finish_attn(*chunks):
+        for c in chunks:
+            put(0, c, state)
+        for r in (slice(n, n + 128) for n in range(0, tokens, 128)):
             square, inner = scale_ref[r, :], center_ref[r, :]
-            for h in (mine(c), others(c)):
-                a = inside[h, r, :] + nn(grown[r, lane(h)], state[h])
+            for h in [h for c in chunks for h in (mine(c), others(c))]:
+                a = inside[h, r, :] + jnp.exp2(cols[h, r, :]) * nn(q[r, lane(h)], state[h])
                 attn[h, r, :] = a
                 square = square + a * a
                 inner = inner + dnorm[h, r, :] * a
@@ -576,6 +573,12 @@
 
     for d in range(1, n_tp):
         tp_copy(d).start()
+
+    @pl.loop(0, heads)
+    def _(h):
+        grow = jnp.exp2(cols[h])
+        grown[:, lane(h)] = (q[:, lane(h)].astype(F32) * grow).astype(BF16)
+
     total = sums[...]
     for d in range(1, n_tp):
         tp_copy(d).wait_recv()
@@ -587,27 +590,28 @@
         scale_ref[r, :] = jnp.broadcast_to(scale[n : n + 1, :], (128, 128)).T
         center_ref[r, :] = jnp.broadcast_to(center[n : n + 1, :], (128, 128)).T
 
-    def pointwise(h):
-        weighted = None
+    def grad_pair(c):
+        for h in (others(c), mine(c)):
+            weighted = None
+            for i in range(nb):
+                r = span_of(i)
+                sc = scale_ref[r, :]
+                g = (sc * (dnorm[h, r, :] - attn[h, r, :] * sc * center_ref[r, :])).astype(BF16)
+                grad[r, lane(h)] = g
+                w = tn(grown[r, lane(h)], g)
+                weighted = w if weighted is None else weighted + w
+            own[1, h] = weighted
+
+    def outputs(h):
         for i in range(nb):
             r = span_of(i)
-            sc = scale_ref[r, :]
-            s, d = sig[h, r, :], dnorm[h, r, :]
-            normed = attn[h, r, :] * sc
-            g = (sc * (d - normed * center_ref[r, :])).astype(BF16)
-            grad[r, lane(h)] = g
+            s = sig[h, r, :]
+            normed = attn[h, r, :] * scale_ref[r, :]
             up[r, lane(h)] = (normed * s).astype(BF16)
-            gate[r, lane(h)] = (d * normed * (1.0 - s)).astype(BF16)
-            w = tn(grown[r, lane(h)], g)
-            weighted = w if weighted is None else weighted + w
-        own[1, h] = weighted
-
-    def pointwise_pair(c):
-        pair = (others(c), mine(c))
-        for h in pair:
-            pointwise(h)
-
-    first_exchange(1, pointwise_pair, 0)
+            gate[r, lane(h)] = (dnorm[h, r, :] * normed * (1.0 - s)).astype(BF16)
+
+    first_exchange(1, grad_pair, 0)
+    pl.loop(0, heads)(outputs)
 
     def backward_pair(c):
         pair = (mine(c), others(c))
@@ -638,7 +642,11 @@
                 dkt[h, :, span_of(j)] = dk[e, j]
                 dvt[h, :, span_of(j)] = dv[e, j]
 
-    ticks(1, backward_pair, lambda c: put(1, c, state_grad))
+    def put_grads(*chunks):
+        for c in chunks:
+            put(1, c, state_grad)
+
+    ticks(1, backward_pair, put_grads)
 
     if crossed:
         for o in range(1, n_seq):

time: 49.1 us -> 48.2 us (0.982)
  Pallas kernels: 48.3 us -> 47.5 us
    pallas_call x1, Pallas kernels: 44.3 us -> 43.5 us  [shards(): pl.pallas_call(functools.partial(kernel, n_seq, n_tp, heads, dim, tokens)...]
where the time goes in v5:
time: 48.2 us; the launch traced here: 48.1 us
  Pallas kernels  47.5 us (99%)
  between operations  0.64 us (1%)
    pallas_call x1, Pallas kernels, shards(): pl.pallas_call(functools.partial(kernel, n_seq, n_tp, heads, dim, tokens)...  43.5 us
    pallas_call x1, Pallas kernels, shards(): pl.pallas_call(functools.partial(last_kernel, heads, dim, tokens), out_sh...  3.96 us

profile of v5, /device:TPU:0, one launch (start us, length us, event | category | flops | bytes accessed | tf_op | source)
XLA Modules:
  0.0 48.1 jit_solution(3517329613045919751)
XLA Ops:
  0.6 43.5 %shard_map.101 = (bf16[512,2048]{1,0:T(8,128)(2,1)S(1)}, bf16[512,2048]{1,0:T(8,128)(2,1)S(1)}, bf16[512,2048]{1,0:T(8,128)(2,1)S(1)}, bf16[512,2048]{1,0:T(8,12...) custom-call(bf16[512,2048]{1,0:T(8,128)(2,1)} %q_hbm.1, ...), custom_call_target="tpu_custom_call" | custom-call | flops 7247757312 | bytes 10485760 | tf_op jit(solution)/shard_map/pallas_call | solution.py:755
  44.1 4.0 %shard_map.102 = (bf16[512,2048]{1,0:T(8,128)(2,1)}, bf16[512,2048]{1,0:T(8,128)(2,1)}, bf16[512,2048]{1,0:T(8,128)(2,1)}, bf16[512,2048]{1,0:T(8,128)(2,1)}, bf16[512,2048]{1,0:T(8,128)(2,1)}) custom-call(bf16[512,2048]{1,0:T(8,128)(2,1)S(1)} %get-tuple-element.14.out_ref, bf16[512,2048]{1,0:T(8,128)(2,1)S(1)} %get-tuple-element.15.gg_ref, ...), custom_call_target="tpu_custom_call" | custom-call | flops 536870912 | bytes 10485760 | tf_op jit(solution)/shard_map/pallas_call | solution.py:790

commit v6 on v5

--- a/solution.py
+++ b/solution.py
@@ -92,9 +92,6 @@
     first_loads = kv_loads(0, soon, 0)
     more_loads = kv_loads(soon, half, 4) if soon < half else []
     rate_load.start()
-    for c in first_loads + more_loads:
-        c.start()
-
     crossed = chips == 2 and half % 2 == 0
     barrier = pltpu.get_barrier_semaphore()
     if crossed:
@@ -107,6 +104,8 @@
         pl.semaphore_signal(
             barrier, inc=1, device_id=(me, lax.rem(z + d, n_tp)), device_id_type=MESH
         )
+    for c in first_loads + more_loads:
+        c.start()
 
     def lane(h):
         return pl.ds(pl.multiple_of(h * dim, dim), dim)
@@ -371,22 +370,17 @@
         fin_copy(d, c).wait_recv()
         target[h] = (row_of(d, 0, 2, h) * far[d, c] + f * other[d, h]).astype(BF16)
 
-    def local_pair(c):
-        pair = (others(c), mine(c))
+    def local(*some):
         scaled = []
-        for h in pair:
+        for h in some:
             last = cols[h, tokens - 1 : tokens, :]
             scaled.append((k[:, lane(h)].astype(F32) * jnp.exp2(last - cols[h])).astype(BF16))
-        for h, x in zip(pair, scaled):
+        for h, x in zip(some, scaled):
             own[0, h] = tn(x, v[:, lane(h)])
 
     def local_and_next(c):
-        local_pair(c)
+        local(others(c), mine(c))
         cols_pair(c + 1 - (c + 1) // half)
-
-    def s0_start(d, c):
-        for h in (others(c), mine(c)):
-            s0_copy(d, h).start()
 
     def levels0(d, lo, hi, lag, body):
         count = 2 if crossed else 1
@@ -399,22 +393,24 @@
                 level0(d, c - lag, (e + lo - lag) % 2 == 1)
 
     def first_exchange(d, body, done):
-        lead = min(2, half)
-
-        @pl.loop(done, lead)
-        def _(c):
-            body(c)
-            s0_start(d, c)
-
+        for n, h in enumerate([others(0), others(1), mine(0), mine(1)]):
+            if n >= done:
+                body(h)
+                s0_copy(d, h).start()
         if d == 0:
+            cols_pair(2 - 2 // half)
             span_step(0)
 
         def more(c):
-            body(c)
-            s0_start(d, c)
-
-        levels0(d, lead, half, lead, more)
-        levels0(d, half, half + lead, lead, lambda c: None)
+            if d == 0:
+                local_and_next(c)
+            else:
+                body(others(c), mine(c))
+            for h in (others(c), mine(c)):
+                s0_copy(d, h).start()
+
+        levels0(d, 2, half, 2, more)
+        levels0(d, half, half + 2, 2, lambda c: None)
         if d == 0:
             span_step(1)
 
@@ -459,19 +455,20 @@
     cols_pair(0)
     for c in first_loads:
         c.wait()
-    local_and_next(0)
+    local(others(0))
     pl.semaphore_wait(barrier, len(others_along) + n_tp - 1)
+    s0_copy(0, others(0)).start()
     if crossed:
         for o in range(1, n_seq):
             last_copy(o).start()
     else:
         sp_copy(0).start()
-    s0_start(0, 0)
+    cols_pair(1)
     for c in more_loads:
         c.wait()
     up_load.start()
     gate_load.start()
-    first_exchange(0, local_and_next, 1)
+    first_exchange(0, local, 1)
 
     tiles = [(i, j) for i in range(nb) for j in range(i + 1)]
     sub = block // dim
@@ -574,11 +571,45 @@
     for d in range(1, n_tp):
         tp_copy(d).start()
 
+    def all_sent(d):
+        for b in (0, 1):
+            part = pl.ds(b * half, half)
+            pltpu.make_async_remote_copy(
+                src_ref=own.at[d, part], dst_ref=other.at[d, part], send_sem=s0_send.at[d],
+                recv_sem=s0_recv.at[d, 0], device_id=partner(0), device_id_type=MESH,
+            ).wait_send()
+
+        def sent_all(s, count):
+            part = pl.ds(0, count)
+            pltpu.make_async_remote_copy(
+                src_ref=sent.at[d, s, part], dst_ref=got.at[d, s, part], send_sem=st_send.at[d, s],
+                recv_sem=st_recv.at[d, s, 0], device_id=partner(s + 1), device_id_type=MESH,
+            ).wait_send()
+
+        if crossed:
+            pl.when(takes(d, 1) == 0)(lambda: sent_all(0, half))
+            pl.when(takes(d, 1) == 1)(lambda: sent_all(0, half // 2))
+        else:
+            for s in range(chips - 1):
+                sent_all(s, half)
+        pl.when(takes(d, chips) == 0)(lambda: sent_all(chips - 1, half))
+        pltpu.make_async_remote_copy(
+            src_ref=edge.at[d], dst_ref=far.at[d], send_sem=fin_send.at[d],
+            recv_sem=fin_recv.at[d, 0], device_id=partner(0), device_id_type=MESH,
+        ).wait_send()
+
     @pl.loop(0, heads)
     def _(h):
         grow = jnp.exp2(cols[h])
         grown[:, lane(h)] = (q[:, lane(h)].astype(F32) * grow).astype(BF16)
 
+    all_sent(0)
+    if crossed:
+        for o in range(1, n_seq):
+            last_copy(o).wait_send()
+    else:
+        for b in range(bits):
+            sp_copy(b).wait_send()
     total = sums[...]
     for d in range(1, n_tp):
         tp_copy(d).wait_recv()
@@ -590,8 +621,8 @@
         scale_ref[r, :] = jnp.broadcast_to(scale[n : n + 1, :], (128, 128)).T
         center_ref[r, :] = jnp.broadcast_to(center[n : n + 1, :], (128, 128)).T
 
-    def grad_pair(c):
-        for h in (others(c), mine(c)):
+    def grads(*some):
+        for h in some:
             weighted = None
             for i in range(nb):
                 r = span_of(i)
@@ -610,7 +641,7 @@
             up[r, lane(h)] = (normed * s).astype(BF16)
             gate[r, lane(h)] = (dnorm[h, r, :] * normed * (1.0 - s)).astype(BF16)
 
-    first_exchange(1, grad_pair, 0)
+    first_exchange(1, grads, 0)
     pl.loop(0, heads)(outputs)
 
     def backward_pair(c):
@@ -648,39 +679,7 @@
 
     ticks(1, backward_pair, put_grads)
 
-    if crossed:
-        for o in range(1, n_seq):
-            last_copy(o).wait_send()
-    else:
-        for b in range(bits):
-            sp_copy(b).wait_send()
-    for d in (0, 1):
-        for b in (0, 1):
-            part = pl.ds(b * half, half)
-            pltpu.make_async_remote_copy(
-                src_ref=own.at[d, part], dst_ref=other.at[d, part], send_sem=s0_send.at[d],
-                recv_sem=s0_recv.at[d, 0], device_id=partner(0), device_id_type=MESH,
-            ).wait_send()
-
-        def sent_all(s, count):
-            part = pl.ds(0, count)
-            pltpu.make_async_remote_copy(
-                src_ref=sent.at[d, s, part], dst_ref=got.at[d, s, part], send_sem=st_send.at[d, s],
-                recv_sem=st_recv.at[d, s, 0], device_id=partner(s + 1), device_id_type=MESH,
-            ).wait_send()
-
-        if crossed:
-            pl.when(takes(d, 1) == 0)(lambda: sent_all(0, half))
-            pl.when(takes(d, 1) == 1)(lambda: sent_all(0, half // 2))
-        else:
-            for s in range(chips - 1):
-                sent_all(s, half)
-        pl.when(takes(d, chips) == 0)(lambda: sent_all(chips - 1, half))
-        pltpu.make_async_remote_copy(
-            src_ref=edge.at[d], dst_ref=far.at[d], send_sem=fin_send.at[d],
-            recv_sem=fin_recv.at[d, 0], device_id=partner(0), device_id_type=MESH,
-        ).wait_send()
-
+    all_sent(1)
     for d in range(1, n_tp):
         tp_copy(d).wait_send()
 

time: 48.2 us -> 48.2 us (level)
  no operation moved by 1% of the time
where the time goes in v6:
time: 48.2 us; the launch traced here: 48.1 us
  Pallas kernels  47.5 us (99%)
  between operations  0.64 us (1%)
    pallas_call x1, Pallas kernels, shards(): pl.pallas_call(functools.partial(kernel, n_seq, n_tp, heads, dim, tokens)...  43.5 us
    pallas_call x1, Pallas kernels, shards(): pl.pallas_call(functools.partial(last_kernel, heads, dim, tokens), out_sh...  3.96 us

profile of v6, /device:TPU:0, one launch (start us, length us, event | category | flops | bytes accessed | tf_op | source)
XLA Modules:
  0.0 48.1 jit_solution(7504859947867522752)
XLA Ops:
  0.6 43.5 %shard_map.101 = (bf16[512,2048]{1,0:T(8,128)(2,1)S(1)}, bf16[512,2048]{1,0:T(8,128)(2,1)S(1)}, bf16[512,2048]{1,0:T(8,128)(2,1)S(1)}, bf16[512,2048]{1,0:T(8,12...) custom-call(bf16[512,2048]{1,0:T(8,128)(2,1)} %q_hbm.1, ...), custom_call_target="tpu_custom_call" | custom-call | flops 7247757312 | bytes 10485760 | tf_op jit(solution)/shard_map/pallas_call | solution.py:754
  44.1 4.0 %shard_map.102 = (bf16[512,2048]{1,0:T(8,128)(2,1)}, bf16[512,2048]{1,0:T(8,128)(2,1)}, bf16[512,2048]{1,0:T(8,128)(2,1)}, bf16[512,2048]{1,0:T(8,128)(2,1)}, bf16[512,2048]{1,0:T(8,128)(2,1)}) custom-call(bf16[512,2048]{1,0:T(8,128)(2,1)S(1)} %get-tuple-element.14.out_ref, bf16[512,2048]{1,0:T(8,128)(2,1)S(1)} %get-tuple-element.15.gg_ref, ...), custom_call_target="tpu_custom_call" | custom-call | flops 536870912 | bytes 10485760 | tf_op jit(solution)/shard_map/pallas_call | solution.py:789

commit v7 on v6

--- a/solution.py
+++ b/solution.py
@@ -82,17 +82,20 @@
     soon = min(2, half)
 
     def kv_loads(lo, hi, at):
-        out = []
-        for start in (lo, half + lo):
-            part = slice(start * dim, (start + hi - lo) * dim)
-            for a, b in ((k_hbm, k), (v_hbm, v)):
-                out.append(load(4 + at + len(out), a.at[:, part], b.at[:, part]))
-        return out
-
-    first_loads = kv_loads(0, soon, 0)
-    more_loads = kv_loads(soon, half, 4) if soon < half else []
+        starts, waits = [], []
+        for n, (a, b) in enumerate(((k_hbm, k), (v_hbm, v))):
+            for start in (lo, half + lo):
+                part = slice(start * dim, (start + hi - lo) * dim)
+                starts.append(load(at + n, a.at[:, part], b.at[:, part]))
+            both = slice(0, 2 * (hi - lo) * dim)
+            waits.append(load(at + n, a.at[:, both], b.at[:, both]))
+        return starts, waits
+
+    first_loads, first_waits = kv_loads(0, soon, 4)
+    more_loads, more_waits = kv_loads(soon, half, 6) if soon < half else ([], [])
     rate_load.start()
     crossed = chips == 2 and half % 2 == 0
+    group = 2 if crossed else 1
     barrier = pltpu.get_barrier_semaphore()
     if crossed:
         others_along = [(lax.rem(me + o, n_seq), z) for o in range(1, n_seq)]
@@ -155,16 +158,36 @@
         )
 
     def last_copy(o):
+        if o == 1:
+            slot = core
+        elif o == n_seq - 1:
+            slot = 1 - core
+        else:
+            slot = 1
         return pltpu.make_async_remote_copy(
-            src_ref=span.at[0], dst_ref=span_in.at[me], send_sem=sp_send.at[o],
-            recv_sem=sp_recv.at[o], device_id=(lax.rem(me + o, n_seq), z), device_id_type=MESH,
-        )
-
-    def s0_copy(d, h):
+            src_ref=span.at[0], dst_ref=span_in.at[me], send_sem=sp_send.at[0],
+            recv_sem=sp_recv.at[slot], device_id=(lax.rem(me + o, n_seq), z), device_id_type=MESH,
+        )
+
+    def lasts(count, slot):
+        part = span_in.at[pl.ds(0, count)]
         return pltpu.make_async_remote_copy(
-            src_ref=own.at[d, h], dst_ref=other.at[d, h], send_sem=s0_send.at[d],
-            recv_sem=s0_recv.at[d, h], device_id=partner(0), device_id_type=MESH,
-        )
+            src_ref=part, dst_ref=part, send_sem=sp_send.at[0], recv_sem=sp_recv.at[slot],
+            device_id=partner(0), device_id_type=MESH,
+        )
+
+    def s0_copy(d, h, slot, count=1):
+        part = pl.ds(h, count)
+        return pltpu.make_async_remote_copy(
+            src_ref=own.at[d, part], dst_ref=other.at[d, part], send_sem=s0_send.at[d],
+            recv_sem=s0_recv.at[d, slot], device_id=partner(0), device_id_type=MESH,
+        )
+
+    def s0_start(d, c, needed):
+        if needed:
+            s0_copy(d, others(c), c).start()
+        else:
+            s0_copy(d, mine(c), half).start()
 
     def st_copy(d, s, c):
         return pltpu.make_async_remote_copy(
@@ -175,7 +198,7 @@
     def fin_copy(d, c):
         return pltpu.make_async_remote_copy(
             src_ref=edge.at[d, c], dst_ref=far.at[d, c], send_sem=fin_send.at[d],
-            recv_sem=fin_recv.at[d, c], device_id=partner(0), device_id_type=MESH,
+            recv_sem=fin_recv.at[d, c // group], device_id=partner(0), device_id_type=MESH,
         )
 
     def set_factors(b, here, there, before):
@@ -204,17 +227,10 @@
 
     def crossed_spans(b):
         if b == 0:
-            o = 1 + (1 - core) * (n_seq - 2)
-            last_copy(o).wait_recv()
+            lasts(1, 0).wait_recv()
             set_factors(0, span[0], span_in[partner(0)[0]], None)
             return
-        for o in range(1, n_seq):
-            if o == 1:
-                pl.when(core == 0)(lambda: last_copy(1).wait_recv())
-            elif o == n_seq - 1:
-                pl.when(core == 1)(lambda: last_copy(n_seq - 1).wait_recv())
-            else:
-                last_copy(o).wait_recv()
+        lasts(n_seq - 2, 1).wait_recv()
 
         def chip(at):
             first = at - lax.rem(at, 2)
@@ -246,7 +262,7 @@
 
     def level0(d, c, crosses):
         h = mine(c)
-        s0_copy(d, h).wait_recv()
+        s0_copy(d, h, c).wait_recv()
         total = row_of(d, 0, 0, h) * own[d, h] + row_of(d, 0, 1, h) * other[d, h]
         if not crossed:
             sent[d, 0, c] = total
@@ -361,14 +377,16 @@
 
         fin_copy(d, c).start()
 
-    def put(d, c, target):
+    def put(d, chunks, target):
         f = takes(d, 0).astype(F32)
-        h = mine(c)
-        target[h] = (row_of(d, 0, 2, h) * edge[d, c] + f * other[d, h]).astype(BF16)
-        h = others(c)
-        s0_copy(d, h).wait_recv()
-        fin_copy(d, c).wait_recv()
-        target[h] = (row_of(d, 0, 2, h) * far[d, c] + f * other[d, h]).astype(BF16)
+        pltpu.make_async_remote_copy(
+            src_ref=edge.at[d, pl.ds(chunks[0], group)], dst_ref=far.at[d, pl.ds(chunks[0], group)],
+            send_sem=fin_send.at[d], recv_sem=fin_recv.at[d, chunks[0] // group],
+            device_id=partner(0), device_id_type=MESH,
+        ).wait_recv()
+        for c in chunks:
+            for h, end in ((mine(c), edge), (others(c), far)):
+                target[h] = (row_of(d, 0, 2, h) * end[d, c] + f * other[d, h]).astype(BF16)
 
     def local(*some):
         scaled = []
@@ -393,10 +411,10 @@
                 level0(d, c - lag, (e + lo - lag) % 2 == 1)
 
     def first_exchange(d, body, done):
-        for n, h in enumerate([others(0), others(1), mine(0), mine(1)]):
+        for n, (c, needed) in enumerate(((0, True), (1, True), (0, False), (1, False))):
             if n >= done:
-                body(h)
-                s0_copy(d, h).start()
+                body(others(c) if needed else mine(c))
+                s0_start(d, c, needed)
         if d == 0:
             cols_pair(2 - 2 // half)
             span_step(0)
@@ -406,13 +424,14 @@
                 local_and_next(c)
             else:
                 body(others(c), mine(c))
-            for h in (others(c), mine(c)):
-                s0_copy(d, h).start()
+            for needed in (True, False):
+                s0_start(d, c, needed)
 
         levels0(d, 2, half, 2, more)
         levels0(d, half, half + 2, 2, lambda c: None)
         if d == 0:
             span_step(1)
+        s0_copy(d, (1 - core) * half, half, half).wait_recv()
 
     def ticks(d, body, finish):
         if crossed:
@@ -453,18 +472,18 @@
                     stage(t - lag)
 
     cols_pair(0)
-    for c in first_loads:
+    for c in first_waits:
         c.wait()
     local(others(0))
     pl.semaphore_wait(barrier, len(others_along) + n_tp - 1)
-    s0_copy(0, others(0)).start()
+    s0_start(0, 0, True)
     if crossed:
         for o in range(1, n_seq):
             last_copy(o).start()
     else:
         sp_copy(0).start()
     cols_pair(1)
-    for c in more_loads:
+    for c in more_waits:
         c.wait()
     up_load.start()
     gate_load.start()
@@ -531,8 +550,7 @@
                 before_norm(h, i)
 
     def finish_attn(*chunks):
-        for c in chunks:
-            put(0, c, state)
+        put(0, chunks, state)
         for r in (slice(n, n + 128) for n in range(0, tokens, 128)):
             square, inner = scale_ref[r, :], center_ref[r, :]
             for h in [h for c in chunks for h in (mine(c), others(c))]:
@@ -564,8 +582,8 @@
 
     def tp_copy(d):
         return pltpu.make_async_remote_copy(
-            src_ref=sums, dst_ref=sums_in.at[d - 1], send_sem=tp_send.at[d - 1],
-            recv_sem=tp_recv.at[d - 1], device_id=(me, lax.rem(z + d, n_tp)), device_id_type=MESH,
+            src_ref=sums, dst_ref=sums_in.at[d - 1], send_sem=tp_send.at[0],
+            recv_sem=tp_recv.at[0], device_id=(me, lax.rem(z + d, n_tp)), device_id_type=MESH,
         )
 
     for d in range(1, n_tp):
@@ -573,11 +591,7 @@
 
     def all_sent(d):
         for b in (0, 1):
-            part = pl.ds(b * half, half)
-            pltpu.make_async_remote_copy(
-                src_ref=own.at[d, part], dst_ref=other.at[d, part], send_sem=s0_send.at[d],
-                recv_sem=s0_recv.at[d, 0], device_id=partner(0), device_id_type=MESH,
-            ).wait_send()
+            s0_copy(d, b * half, 0, half).wait_send()
 
         def sent_all(s, count):
             part = pl.ds(0, count)
@@ -605,14 +619,18 @@
 
     all_sent(0)
     if crossed:
-        for o in range(1, n_seq):
-            last_copy(o).wait_send()
+        lasts(n_seq - 1, 0).wait_send()
     else:
         for b in range(bits):
             sp_copy(b).wait_send()
     total = sums[...]
+    every = pltpu.make_async_remote_copy(
+        src_ref=sums_in, dst_ref=sums_in, send_sem=tp_send.at[0], recv_sem=tp_recv.at[0],
+        device_id=partner(0), device_id_type=MESH,
+    )
+    if n_tp > 1:
+        every.wait_recv()
     for d in range(1, n_tp):
-        tp_copy(d).wait_recv()
         total = total + sums_in[d - 1]
     scale = lax.rsqrt(total[0:strips] / width + 1e-06)
     center = total[strips : 2 * strips] * scale / width
@@ -674,14 +692,13 @@
                 dvt[h, :, span_of(j)] = dv[e, j]
 
     def put_grads(*chunks):
-        for c in chunks:
-            put(1, c, state_grad)
+        put(1, chunks, state_grad)
 
     ticks(1, backward_pair, put_grads)
 
     all_sent(1)
-    for d in range(1, n_tp):
-        tp_copy(d).wait_send()
+    if n_tp > 1:
+        every.wait_send()
 
 
 def last_kernel(
@@ -743,7 +760,9 @@
         tile = (dim, dim)
         dma = pltpu.SemaphoreType.DMA
         peers = max(n_tp - 1, 1)
-        spans = n_seq if chips == 2 else bits
+        crossed = chips == 2 and half % 2 == 0
+        spans = 2 if crossed else bits
+        ends = half // 2 if crossed else half
         sums = (-(-2 * (tokens // 128) // 8) * 8, 128)
         hbm = pl.BlockSpec(memory_space=pltpu.HBM)
         vmem = pl.BlockSpec(memory_space=pltpu.VMEM)
@@ -774,9 +793,9 @@
                 pltpu.VMEM((2, bits + 1, 3, heads, dim), F32),
                 pltpu.VMEM(sums, F32), pltpu.VMEM((peers, *sums), F32),
                 pltpu.VMEM((tokens, dim), F32), pltpu.VMEM((tokens, dim), F32),
-                dma((12,)), dma((spans,)), dma((spans,)), dma((2,)), dma((2, heads)),
-                dma((2, chips)), dma((2, chips, half)), dma((2,)), dma((2, half)),
-                dma((peers,)), dma((peers,)),
+                dma((8,)), dma((spans,)), dma((spans,)), dma((2,)), dma((2, half + 1)),
+                dma((2, chips)), dma((2, chips, half)), dma((2,)), dma((2, ends)),
+                dma((1,)), dma((1,)),
             ],
             compiler_params=pltpu.CompilerParams(
                 collective_id=0, has_side_effects=True, vmem_limit_bytes=43 << 20

time: 48.2 us -> 47.9 us (level)
  no operation moved by 1% of the time
where the time goes in v7:
time: 47.9 us; the launch traced here: 47.8 us
  Pallas kernels  47.1 us (98%)
  between operations  0.64 us (1%)
    pallas_call x1, Pallas kernels, shards(): pl.pallas_call(functools.partial(kernel, n_seq, n_tp, heads, dim, tokens)...  43.2 us
    pallas_call x1, Pallas kernels, shards(): pl.pallas_call(functools.partial(last_kernel, heads, dim, tokens), out_sh...  3.96 us

profile of v7, /device:TPU:0, one launch (start us, length us, event | category | flops | bytes accessed | tf_op | source)
XLA Modules:
  0.0 47.8 jit_solution(5970788638087764704)
XLA Ops:
  0.6 43.2 %shard_map.101 = (bf16[512,2048]{1,0:T(8,128)(2,1)S(1)}, bf16[512,2048]{1,0:T(8,128)(2,1)S(1)}, bf16[512,2048]{1,0:T(8,128)(2,1)S(1)}, bf16[512,2048]{1,0:T(8,12...) custom-call(bf16[512,2048]{1,0:T(8,128)(2,1)} %q_hbm.1, ...), custom_call_target="tpu_custom_call" | custom-call | flops 7247757312 | bytes 10485760 | tf_op jit(solution)/shard_map/pallas_call | solution.py:773
  43.8 4.0 %shard_map.102 = (bf16[512,2048]{1,0:T(8,128)(2,1)}, bf16[512,2048]{1,0:T(8,128)(2,1)}, bf16[512,2048]{1,0:T(8,128)(2,1)}, bf16[512,2048]{1,0:T(8,128)(2,1)}, bf16[512,2048]{1,0:T(8,128)(2,1)}) custom-call(bf16[512,2048]{1,0:T(8,128)(2,1)S(1)} %get-tuple-element.14.out_ref, bf16[512,2048]{1,0:T(8,128)(2,1)S(1)} %get-tuple-element.15.gg_ref, ...), custom_call_target="tpu_custom_call" | custom-call | flops 536870912 | bytes 10485760 | tf_op jit(solution)/shard_map/pallas_call | solution.py:808

commit v8 on v7

--- a/solution.py
+++ b/solution.py
@@ -396,19 +396,8 @@
         for h, x in zip(some, scaled):
             own[0, h] = tn(x, v[:, lane(h)])
 
-    def local_and_next(c):
-        local(others(c), mine(c))
-        cols_pair(c + 1 - (c + 1) // half)
-
-    def levels0(d, lo, hi, lag, body):
-        count = 2 if crossed else 1
-
-        @pl.loop(0, (hi - lo) // count)
-        def _(n):
-            for e in range(count):
-                c = lo + n * count + e
-                body(c)
-                level0(d, c - lag, (e + lo - lag) % 2 == 1)
+    def next_cols(c):
+        cols_pair(c - (c // half) * (c - half + 1))
 
     def first_exchange(d, body, done):
         for n, (c, needed) in enumerate(((0, True), (1, True), (0, False), (1, False))):
@@ -416,21 +405,29 @@
                 body(others(c) if needed else mine(c))
                 s0_start(d, c, needed)
         if d == 0:
-            cols_pair(2 - 2 // half)
+            for c in range(group):
+                next_cols(2 + c)
             span_step(0)
 
-        def more(c):
+        @pl.loop(0, (half - 2) // group)
+        def _(n):
+            some = [2 + n * group + e for e in range(group)]
+            body(*(h for c in some for h in (others(c), mine(c))))
             if d == 0:
-                local_and_next(c)
-            else:
-                body(others(c), mine(c))
+                for c in some:
+                    next_cols(c + group)
             for needed in (True, False):
-                s0_start(d, c, needed)
-
-        levels0(d, 2, half, 2, more)
-        levels0(d, half, half + 2, 2, lambda c: None)
+                for c in some:
+                    s0_start(d, c, needed)
+            for e, c in enumerate(some):
+                level0(d, c - 2, e == 1)
+
         if d == 0:
             span_step(1)
+
+    def last_levels0(d):
+        for e, c in enumerate((half - 2, half - 1)):
+            level0(d, c, e == 1)
         s0_copy(d, (1 - core) * half, half, half).wait_recv()
 
     def ticks(d, body, finish):
@@ -459,6 +456,10 @@
             @pl.when(t < half)
             def _():
                 body(t)
+
+            @pl.when(t == 0)
+            def _():
+                last_levels0(d)
 
             for n, (lag, stage) in enumerate(stages):
                 if d == 0 and 1 <= n + 1 < bits and n >= 1 and not crossed:

time: 47.9 us -> 47.8 us (level)
  no operation moved by 1% of the time
where the time goes in v8:
time: 47.8 us; the launch traced here: 47.7 us
  Pallas kernels  47 us (98%)
  between operations  0.64 us (1%)
    pallas_call x1, Pallas kernels, shards(): pl.pallas_call(functools.partial(kernel, n_seq, n_tp, heads, dim, tokens)...  43.1 us
    pallas_call x1, Pallas kernels, shards(): pl.pallas_call(functools.partial(last_kernel, heads, dim, tokens), out_sh...  3.96 us

profile of v8, /device:TPU:0, one launch (start us, length us, event | category | flops | bytes accessed | tf_op | source)
XLA Modules:
  0.0 47.7 jit_solution(1678613096407512752)
XLA Ops:
  0.6 43.1 %shard_map.101 = (bf16[512,2048]{1,0:T(8,128)(2,1)S(1)}, bf16[512,2048]{1,0:T(8,128)(2,1)S(1)}, bf16[512,2048]{1,0:T(8,128)(2,1)S(1)}, bf16[512,2048]{1,0:T(8,12...) custom-call(bf16[512,2048]{1,0:T(8,128)(2,1)} %q_hbm.1, ...), custom_call_target="tpu_custom_call" | custom-call | flops 7247757312 | bytes 10485760 | tf_op jit(solution)/shard_map/pallas_call | solution.py:774
  43.7 4.0 %shard_map.102 = (bf16[512,2048]{1,0:T(8,128)(2,1)}, bf16[512,2048]{1,0:T(8,128)(2,1)}, bf16[512,2048]{1,0:T(8,128)(2,1)}, bf16[512,2048]{1,0:T(8,128)(2,1)}, bf16[512,2048]{1,0:T(8,128)(2,1)}) custom-call(bf16[512,2048]{1,0:T(8,128)(2,1)S(1)} %get-tuple-element.14.out_ref, bf16[512,2048]{1,0:T(8,128)(2,1)S(1)} %get-tuple-element.15.gg_ref, ...), custom_call_target="tpu_custom_call" | custom-call | flops 536870912 | bytes 10485760 | tf_op jit(solution)/shard_map/pallas_call | solution.py:809

commit v9 on v8

--- a/solution.py
+++ b/solution.py
@@ -409,8 +409,7 @@
                 next_cols(2 + c)
             span_step(0)
 
-        @pl.loop(0, (half - 2) // group)
-        def _(n):
+        def block_of(n):
             some = [2 + n * group + e for e in range(group)]
             body(*(h for c in some for h in (others(c), mine(c))))
             if d == 0:
@@ -419,7 +418,17 @@
             for needed in (True, False):
                 for c in some:
                     s0_start(d, c, needed)
-            for e, c in enumerate(some):
+            return some
+
+        ahead = d == 0 and crossed
+        if ahead:
+            level0(d, 0, False)
+            level0(d, 1, True)
+            block_of(0)
+
+        @pl.loop(1 if ahead else 0, (half - 2) // group)
+        def _(n):
+            for e, c in enumerate(block_of(n)):
                 level0(d, c - 2, e == 1)
 
         if d == 0:
@@ -799,7 +808,7 @@
                 dma((1,)), dma((1,)),
             ],
             compiler_params=pltpu.CompilerParams(
-                collective_id=0, has_side_effects=True, vmem_limit_bytes=43 << 20
+                collective_id=0, has_side_effects=True, vmem_limit_bytes=44 << 20
             ),
             cost_estimate=pl.CostEstimate(
                 flops=flops, bytes_accessed=tokens * flat * 10, transcendentals=0

time: 47.8 us -> 48.1 us (level)
  no operation moved by 1% of the time
where the time goes in v9:
time: 48.1 us; the launch traced here: 47.9 us
  Pallas kernels  47.3 us (98%)
  between operations  0.64 us (1%)
    pallas_call x1, Pallas kernels, shards(): pl.pallas_call(functools.partial(kernel, n_seq, n_tp, heads, dim, tokens)...  43.3 us
    pallas_call x1, Pallas kernels, shards(): pl.pallas_call(functools.partial(last_kernel, heads, dim, tokens), out_sh...  3.96 us

profile of v9, /device:TPU:0, one launch (start us, length us, event | category | flops | bytes accessed | tf_op | source)
XLA Modules:
  0.0 47.9 jit_solution(15125607390656680626)
XLA Ops:
  0.6 43.3 %shard_map.101 = (bf16[512,2048]{1,0:T(8,128)(2,1)S(1)}, bf16[512,2048]{1,0:T(8,128)(2,1)S(1)}, bf16[512,2048]{1,0:T(8,128)(2,1)S(1)}, bf16[512,2048]{1,0:T(8,12...) custom-call(bf16[512,2048]{1,0:T(8,128)(2,1)} %q_hbm.1, ...), custom_call_target="tpu_custom_call" | custom-call | flops 7247757312 | bytes 10485760 | tf_op jit(solution)/shard_map/pallas_call | solution.py:783
  44.0 4.0 %shard_map.102 = (bf16[512,2048]{1,0:T(8,128)(2,1)}, bf16[512,2048]{1,0:T(8,128)(2,1)}, bf16[512,2048]{1,0:T(8,128)(2,1)}, bf16[512,2048]{1,0:T(8,128)(2,1)}, bf16[512,2048]{1,0:T(8,128)(2,1)}) custom-call(bf16[512,2048]{1,0:T(8,128)(2,1)S(1)} %get-tuple-element.14.out_ref, bf16[512,2048]{1,0:T(8,128)(2,1)S(1)} %get-tuple-element.15.gg_ref, ...), custom_call_target="tpu_custom_call" | custom-call | flops 536870912 | bytes 10485760 | tf_op jit(solution)/shard_map/pallas_call | solution.py:818
